TPU v7x, 32 devices: a whole 2x2x4 slice. The times are simulated.
32 devices in a mesh: shard: 8 (over y, x, core), head: 4 (over z).
Axes of the slice: x: 2, y: 2, z: 4, core: 2. Of those that a mesh axis runs over, the one named last changes fastest.
Arguments:
- block_in: bfloat16 [4, 4096, 768], P(None, ('shard', 'head')), may hold values from -6 to 6
- gain_in: float32 [768], replicated, may hold values from 0.5 to 1.5
- w_in: bfloat16 [768, 3352], P(('shard', 'head')), may hold values from -0.21875 to 0.21875
- conv_w: float32 [4, 1792], replicated, may hold values from -3 to 3
- conv_b: float32 [1792], replicated, may hold values from -3 to 3
- dt_bias: float32 [24], replicated, may hold values from -4.5 to 1
- a_log: float32 [24], replicated, may hold values from -12 to 0
- d_skip: float32 [24], replicated, may hold values from 0.5 to 1.5
- gain_out: float32 [1536], replicated, may hold values from 0.5 to 1.5
- w_out: bfloat16 [1536, 768], P(('shard', 'head')), may hold values from -0.15625 to 0.15625
- out_grad: bfloat16 [4, 4096, 768], P(None, ('shard', 'head')), may hold values from -6 to 6
Outputs:
- block_out: bfloat16 [4, 4096, 768], P(None, ('shard', 'head'))
- in_grad: float32 [4, 4096, 768], P(None, ('shard', 'head'))
- gain_in_grad: float32 [768], replicated
- w_in_grad: float32 [768, 3352], P(('shard', 'head'))
- conv_w_grad: float32 [4, 1792], replicated
- conv_b_grad: float32 [1792], replicated
- dt_bias_grad: float32 [24], replicated
- a_log_grad: float32 [24], replicated
- d_skip_grad: float32 [24], replicated
- gain_out_grad: float32 [1536], replicated
- w_out_grad: float32 [1536, 768], P(('shard', 'head'))
All inputs are finite; a program needn't handle non-finite values.
Results may differ from a plain program's by a relative error of at most 0.011.
Values may be sent and summed in bfloat16 or wider, within the bound.
A program may use at most 192 MiB of HBM per device.

v0:
```python
import jax
import jax.numpy as jnp
from jax import lax
from jax.sharding import PartitionSpec as P

BLOCK = 256


EPSILON = 1e-05
HIGHEST = lax.Precision.HIGHEST


def shifted(block, axis, distance):
    devices = range(lax.axis_size(axis))
    route = [(i - distance, i) for i in devices if i - distance in devices]
    return lax.ppermute(block, axis, route)


def entering_2(array, axis, combine, identity, reverse):
    count, index = (lax.axis_size(axis), lax.axis_index(axis))
    everything = jax.tree.map(lambda part: lax.all_gather(part, axis), array)
    start = jax.tree.map(
        lambda part, zero: jnp.broadcast_to(jnp.asarray(zero, part.dtype), part.shape),
        array,
        identity,
    )

    def lap(k, before):
        at = count - 1 - k if reverse else k
        reached = at > index if reverse else at < index
        new = combine(before, jax.tree.map(lambda part: part[at], everything))
        return jax.tree.map(lambda a, b: jnp.where(reached, a, b), new, before)

    return lax.fori_loop(0, count, lap, start)


def silu_slope(values):
    logistic = jax.nn.sigmoid(values)
    return logistic * (1.0 + values * (1.0 - logistic))


def block_scan(x_heads, b_rows, c_rows, step_rates, deltas, initial, block_size):
    length, head_count, head_dim = x_heads.shape
    block_count = length // block_size
    causal = jnp.arange(block_size)[:, None] >= jnp.arange(block_size)[None, :]

    def advance(carried, sliced):
        x_block, b_block, c_block, delta_block, rate_block = sliced
        running = jnp.cumsum(rate_block, axis=0)
        spread = running[:, None, :] - running[None, :, :]
        decay_matrix = jnp.exp(jnp.where(causal[:, :, None], spread, -jnp.inf))
        scores = jnp.dot(c_block, b_block.T, precision=HIGHEST)
        mixing = scores[:, :, None] * decay_matrix * delta_block[None, :, :]
        inside = jnp.einsum("tsh,shp->thp", mixing, x_block, precision=HIGHEST)
        from_state = (
            jnp.einsum("tn,hpn->thp", c_block, carried, precision=HIGHEST)
            * jnp.exp(running)[:, :, None]
        )
        last_rate = running[-1]
        tail_weights = jnp.exp(last_rate[None, :] - running) * delta_block
        updated = carried * jnp.exp(last_rate)[:, None, None] + jnp.einsum(
            "sh,shp,sn->hpn", tail_weights, x_block, b_block, precision=HIGHEST
        )
        return (updated, inside + from_state)

    blocks = (
        x_heads.reshape(block_count, block_size, head_count, head_dim),
        b_rows.reshape(block_count, block_size, -1),
        c_rows.reshape(block_count, block_size, -1),
        deltas.reshape(block_count, block_size, head_count),
        step_rates.reshape(block_count, block_size, head_count),
    )
    final_state, outputs = lax.scan(advance, initial, blocks)
    return (outputs.reshape(length, head_count, head_dim), final_state)


def causal_conv(padded, taps_weight, bias, length):
    summed = jnp.zeros((length, padded.shape[1]), jnp.float32) + bias[None, :]
    for offset in range(taps_weight.shape[0]):
        summed = summed + taps_weight[offset][None, :] * padded[offset : offset + length]
    return summed


def mixer_local(
    padded_x,
    padded_bc,
    dt_in,
    weight_x,
    bias_x,
    weight_bc,
    bias_bc,
    bias_dt,
    log_rate,
    skip_gain,
    initial,
    block_size,
):
    length, head_count = dt_in.shape
    x_act = jax.nn.silu(causal_conv(padded_x, weight_x, bias_x, length))
    bc_act = jax.nn.silu(causal_conv(padded_bc, weight_bc, bias_bc, length))
    state_size = bc_act.shape[1] // 2
    b_rows = bc_act[:, :state_size]
    c_rows = bc_act[:, state_size:]
    deltas = jax.nn.softplus(dt_in + bias_dt[None, :])
    step_rates = deltas * (-jnp.exp(log_rate))[None, :]
    x_heads = x_act.reshape(length, head_count, -1)
    outputs, final_state = block_scan(
        x_heads, b_rows, c_rows, step_rates, deltas, initial, block_size
    )
    outputs = outputs + skip_gain[None, :, None] * x_heads
    return (outputs, final_state, jnp.cumsum(step_rates, axis=0), c_rows)


def chain_combine(earlier, later):
    return (earlier[0] * later[0], later[1] + later[0][..., None, None] * earlier[1])


def shards(
    block_in, gain_in, w_in, conv_w, conv_b, dt_bias, a_log, d_skip, gain_out, w_out, out_grad
):
    groups = lax.axis_size("head")
    head_index = lax.axis_index("head")
    seqs_dev, segment, model_width = block_in.shape
    inner_width = gain_out.shape[0]
    head_count = dt_bias.shape[0]
    heads_dev = head_count // groups
    head_dim = inner_width // head_count
    inner_dev = inner_width // groups
    state_size = (conv_b.shape[0] - inner_width) // 2
    conv_taps = conv_w.shape[0]
    margin = conv_taps - 1
    row_count = seqs_dev * segment
    full_in, full_out = (
        lax.all_gather(w_in, ("shard", "head"), axis=0, tiled=True),
        lax.all_gather(w_out, ("shard", "head"), axis=0, tiled=True),
    )
    tokens_f = block_in.astype(jnp.float32).reshape(row_count, model_width)
    rms_in = lax.rsqrt(jnp.mean(tokens_f * tokens_f, axis=-1, keepdims=True) + EPSILON)
    normed = (tokens_f * rms_in * gain_in[None, :]).astype(jnp.bfloat16)
    projected = jnp.dot(normed, full_in, preferred_element_type=jnp.float32)
    gate_in = projected[:, :inner_width].astype(jnp.bfloat16)
    x_raw = (
        projected[:, inner_width : 2 * inner_width]
        .astype(jnp.bfloat16)
        .reshape(seqs_dev, segment, inner_width)
    )
    bc_raw = (
        projected[:, 2 * inner_width : 2 * inner_width + 2 * state_size]
        .astype(jnp.bfloat16)
        .reshape(seqs_dev, segment, 2 * state_size)
    )
    dt_raw = (
        projected[:, 2 * inner_width + 2 * state_size :]
        .astype(jnp.bfloat16)
        .reshape(seqs_dev, segment, head_count)
    )
    x_local, dt_local = (
        lax.all_to_all(x_raw, "head", split_axis=2, concat_axis=1, tiled=True),
        lax.all_to_all(dt_raw, "head", split_axis=2, concat_axis=1, tiled=True),
    )
    bc_local = lax.all_gather(bc_raw, "head", axis=1, tiled=True)
    x_prior, bc_prior = shifted((x_local[:, -margin:], bc_local[:, -margin:]), "shard", 1)
    padded_x = jnp.concatenate([x_prior, x_local], axis=1).astype(jnp.float32)
    padded_bc = jnp.concatenate([bc_prior, bc_local], axis=1).astype(jnp.float32)
    dt_in = dt_local.astype(jnp.float32)
    weight_x = lax.dynamic_slice_in_dim(conv_w, head_index * inner_dev, inner_dev, 1)
    bias_x = lax.dynamic_slice_in_dim(conv_b, head_index * inner_dev, inner_dev, 0)
    weight_bc = conv_w[:, inner_width:]
    bias_bc = conv_b[inner_width:]
    bias_dt = lax.dynamic_slice_in_dim(dt_bias, head_index * heads_dev, heads_dev, 0)
    log_rate = lax.dynamic_slice_in_dim(a_log, head_index * heads_dev, heads_dev, 0)
    skip_local = lax.dynamic_slice_in_dim(d_skip, head_index * heads_dev, heads_dev, 0)
    zero_state = jnp.zeros((heads_dev, head_dim, state_size), jnp.float32)

    def local_forward(padded_x_one, padded_bc_one, dt_one):
        return mixer_local(
            padded_x_one,
            padded_bc_one,
            dt_one,
            weight_x,
            bias_x,
            weight_bc,
            bias_bc,
            bias_dt,
            log_rate,
            skip_local,
            zero_state,
            BLOCK,
        )

    mixed_local, final_local, running, c_rows = jax.vmap(local_forward)(padded_x, padded_bc, dt_in)
    decays = jnp.exp(running[:, -1])
    identity = (jnp.ones_like(decays), jnp.zeros_like(final_local))
    entering = entering_2((decays, final_local), "shard", chain_combine, identity, False)[1]
    carried = (
        jnp.einsum("srn,shpn->srhp", c_rows, entering, precision=HIGHEST)
        * jnp.exp(running)[..., None]
    )
    mixed = (mixed_local + carried).reshape(seqs_dev, -1, inner_dev).astype(jnp.bfloat16)
    mixed_tok = lax.all_to_all(mixed, "head", split_axis=1, concat_axis=2, tiled=True).reshape(
        row_count, inner_width
    )
    mixed_f = mixed_tok.astype(jnp.float32)
    gate_f = gate_in.astype(jnp.float32)
    gated_out = mixed_f * jax.nn.silu(gate_f)
    rms_out = lax.rsqrt(jnp.mean(gated_out * gated_out, axis=-1, keepdims=True) + EPSILON)
    gnormed = (gated_out * rms_out * gain_out[None, :]).astype(jnp.bfloat16)
    block_out = (tokens_f + jnp.dot(gnormed, full_out, preferred_element_type=jnp.float32)).astype(
        jnp.bfloat16
    )
    cotangent = out_grad.reshape(row_count, model_width)
    grad_gnormed = lax.dot_general(
        cotangent, full_out, (((1,), (1,)), ((), ())), preferred_element_type=jnp.float32
    )
    grad_w_out = lax.dot_general(
        gnormed, cotangent, (((0,), (0,)), ((), ())), preferred_element_type=jnp.float32
    )
    grad_gain_out = jnp.sum(grad_gnormed * gated_out * rms_out, axis=0)
    scaled_out = grad_gnormed * gain_out[None, :]
    grad_gated = rms_out * scaled_out - gated_out * rms_out**3 * jnp.mean(
        gated_out * scaled_out, axis=-1, keepdims=True
    )
    grad_mixed = (
        (grad_gated * jax.nn.silu(gate_f))
        .astype(jnp.bfloat16)
        .reshape(seqs_dev, segment, inner_width)
    )
    grad_gate = grad_gated * mixed_f * silu_slope(gate_f)
    mixed_back = lax.all_to_all(grad_mixed, "head", split_axis=2, concat_axis=1, tiled=True)
    mixed_back_f = mixed_back.astype(jnp.float32).reshape(seqs_dev, -1, heads_dev, head_dim)
    direct = jnp.einsum(
        "srh,srhp,srn->shpn", jnp.exp(running), mixed_back_f, c_rows, precision=HIGHEST
    )
    leaving = entering_2((decays, direct), "shard", chain_combine, identity, True)[1]

    def local_backward(sliced):
        padded_x_one, padded_bc_one, dt_one, start_state, cot_out, cot_state = sliced

        def run_mixer(
            px_in,
            pbc_in,
            dt_value,
            weight_x_in,
            bias_x_in,
            weight_bc_in,
            bias_bc_in,
            bias_dt_in,
            log_rate_in,
            skip_in,
        ):
            outputs = mixer_local(
                px_in,
                pbc_in,
                dt_value,
                weight_x_in,
                bias_x_in,
                weight_bc_in,
                bias_bc_in,
                bias_dt_in,
                log_rate_in,
                skip_in,
                start_state,
                BLOCK,
            )
            return (outputs[0], outputs[1])

        pullback = jax.vjp(
            run_mixer,
            padded_x_one,
            padded_bc_one,
            dt_one,
            weight_x,
            bias_x,
            weight_bc,
            bias_bc,
            bias_dt,
            log_rate,
            skip_local,
        )[1]
        return pullback((cot_out, cot_state))

    pulled = lax.map(local_backward, (padded_x, padded_bc, dt_in, entering, mixed_back_f, leaving))
    grad_padded_x = pulled[0]
    grad_padded_bc = pulled[1]
    grad_dt = pulled[2]
    param_grads = [jnp.sum(stacked, axis=0) for stacked in pulled[3:]]
    sent_x, sent_bc = shifted((grad_padded_x[:, :margin], grad_padded_bc[:, :margin]), "shard", -1)
    grad_x_range = jnp.concatenate(
        [grad_padded_x[:, margin:-margin], grad_padded_x[:, -margin:] + sent_x], axis=1
    )
    grad_bc_range = jnp.concatenate(
        [grad_padded_bc[:, margin:-margin], grad_padded_bc[:, -margin:] + sent_bc], axis=1
    )
    bc_rounded = lax.optimization_barrier(grad_bc_range.astype(jnp.bfloat16))
    stacked_bc = bc_rounded.reshape(seqs_dev, groups * segment, 1, 2 * state_size)
    pieces = lax.all_to_all(stacked_bc, "head", split_axis=1, concat_axis=2, tiled=True)
    grad_bc_tok = jnp.sum(pieces.astype(jnp.float32), axis=2)
    grad_x_tok, grad_dt_tok = (
        lax.all_to_all(
            grad_x_range.astype(jnp.bfloat16), "head", split_axis=1, concat_axis=2, tiled=True
        ),
        lax.all_to_all(
            grad_dt.astype(jnp.bfloat16), "head", split_axis=1, concat_axis=2, tiled=True
        ),
    )
    grad_proj = jnp.concatenate(
        [
            grad_gate.astype(jnp.bfloat16),
            grad_x_tok.reshape(row_count, inner_width),
            grad_bc_tok.reshape(row_count, 2 * state_size).astype(jnp.bfloat16),
            grad_dt_tok.reshape(row_count, head_count),
        ],
        axis=1,
    )
    grad_w_in = lax.dot_general(
        normed, grad_proj, (((0,), (0,)), ((), ())), preferred_element_type=jnp.float32
    )
    grad_normed = lax.dot_general(
        grad_proj, full_in, (((1,), (1,)), ((), ())), preferred_element_type=jnp.float32
    )
    grad_gain_in = jnp.sum(grad_normed * tokens_f * rms_in, axis=0)
    scaled_in = grad_normed * gain_in[None, :]
    in_grad = (
        out_grad.astype(jnp.float32).reshape(row_count, model_width)
        + rms_in * scaled_in
        - tokens_f * rms_in**3 * jnp.mean(tokens_f * scaled_in, axis=-1, keepdims=True)
    )
    grad_conv_w = jnp.zeros(conv_w.shape, jnp.float32)
    grad_conv_w = lax.dynamic_update_slice_in_dim(
        grad_conv_w, param_grads[0], head_index * inner_dev, 1
    )
    grad_conv_w = grad_conv_w.at[:, inner_width:].set(param_grads[2])
    grad_conv_b = jnp.zeros(conv_b.shape, jnp.float32)
    grad_conv_b = lax.dynamic_update_slice_in_dim(
        grad_conv_b, param_grads[1], head_index * inner_dev, 0
    )
    grad_conv_b = grad_conv_b.at[inner_width:].set(param_grads[3])
    grad_dt_bias = lax.dynamic_update_slice_in_dim(
        jnp.zeros(dt_bias.shape, jnp.float32), param_grads[4], head_index * heads_dev, 0
    )
    grad_a_log = lax.dynamic_update_slice_in_dim(
        jnp.zeros(a_log.shape, jnp.float32), param_grads[5], head_index * heads_dev, 0
    )
    grad_d_skip = lax.dynamic_update_slice_in_dim(
        jnp.zeros(d_skip.shape, jnp.float32), param_grads[6], head_index * heads_dev, 0
    )
    owned_in, owned_out = (
        lax.psum_scatter(grad_w_in, ("shard", "head"), scatter_dimension=0, tiled=True),
        lax.psum_scatter(grad_w_out, ("shard", "head"), scatter_dimension=0, tiled=True),
    )
    summed_small = lax.psum(
        (
            grad_gain_in,
            grad_gain_out,
            grad_conv_w,
            grad_conv_b,
            grad_dt_bias,
            grad_a_log,
            grad_d_skip,
        ),
        ("shard", "head"),
    )
    return (
        block_out.reshape(seqs_dev, segment, model_width),
        in_grad.reshape(seqs_dev, segment, model_width),
        summed_small[0],
        owned_in,
        summed_small[2],
        summed_small[3],
        summed_small[4],
        summed_small[5],
        summed_small[6],
        summed_small[1],
        owned_out,
    )


def solution(mesh):
    placed = (
        P(None, ("shard", "head"), None),
        P(),
        P(("shard", "head"), None),
        P(),
        P(),
        P(),
        P(),
        P(),
        P(),
        P(("shard", "head"), None),
        P(None, ("shard", "head"), None),
    )
    return jax.shard_map(
        shards,
        mesh=mesh,
        in_specs=placed,
        out_specs=(
            P(None, ("shard", "head"), None),
            P(None, ("shard", "head"), None),
            P(),
            P(("shard", "head"), None),
            P(),
            P(),
            P(),
            P(),
            P(),
            P(),
            P(("shard", "head"), None),
        ),
        check_vma=False,
    )
```

profile of v0, /device:TPU:0, one launch (start us, length us, event | category | flops | bytes accessed | tf_op | source)
XLA Modules:
  0.0 1441.7 jit_solution(2255425780823253697)
XLA Ops:
  12.7 66.5 %all-gather.9.cloned.1.call-done = bf16[768,3352]{1,0:T(8,128)(2,1)} async-done(((bf16[24,3352]{1,0:T(8,128)(2,1)}), bf16[768,3352]{1,0:T(8,128)(2,1)}) %all-gather.9.cloned.1.call-update) | async-done | bytes 5148688 | tf_op jit(solution)/shard_map/all_gather | solution.py:134
  79.2 5.6 convolution_convert_fusion
  103.8 24.0 %all-gather.11.cloned.1.call-done = bf16[4,512,256]{2,1,0:T(8,128)(2,1)} async-done(((bf16[4,128,256]{2,1,0:T(8,128)(2,1)}), bf16[4,512,256]{2,1,0:T(8,128)(2,1)}) %all-gather.11.cloned.1.call-update) | async-done | bytes 1048592 | tf_op jit(solution)/shard_map/all_gather | solution.py:161
  136.2 11.9 all-to-all-done.1
  163.9 5.2 reshape.995
  169.1 47.3 %while.212 = (s32[]{:T(128)}, f32[4,6,64,128]{3,2,1,0:T(8,128)S(1)}, f32[2,4,256,6,64]{2,4,3,1,0:T(8,128)}, f32[2,4,256,6]{2,0,3,1:T(2,128)S(1)}, f32[2,4,256,6]...) while((s32[]{:T(128)}, f32[4,6,64,128]{3,2,1,0:T(8,128)S(1)}, ...), condition=%wide.region_4.5_spmd.clone, body=%wide.region_1.4_spmd.clone.sunk | while | flops 2827694080 | bytes 43769544 | solution.py:73
  169.4 7.2 reduce-window.68
  182.2 7.1 fusion.298
  192.9 7.2 reduce-window.68
  205.7 7.1 fusion.298
  218.2 7.2 reduce-window.52
  226.8 15.1 %all-gather.1 = f32[32,1,6]{2,1,0:T(1,128)S(1)} all-gather(f32[4,1,6]{2,1,0:T(1,128)S(1)} %bitcast.928), channel_id=3, replica_groups=mesh['shard'=8,'head'=4] {'shard'}, dimensions={0}, use_global_device_ids=true | all-gather | bytes 864 | tf_op jit(solution)/shard_map/all_gather | solution.py:21
  246.4 20.5 %all-gather.15.cloned.1.call-done = f32[32,6,64,128]{3,2,1,0:T(8,128)} async-done(((f32[4,6,64,128]{3,2,1,0:T(8,128)}), f32[32,6,64,128]{3,2,1,0:T(8,128)}) %all-gather.15.cloned.1.call-update) | async-done | bytes 6291472 | tf_op jit(solution)/shard_map/all_gather | solution.py:21
  266.9 19.3 %while.213 = (s32[]{:T(128)}, f32[4,6,64,128]{3,2,1,0:T(8,128)}, s32[]{:T(128)}, f32[8,4,6,64,128]{4,3,2,1,0:T(8,128)}, f32[8,4,6]{2,1,0:T(4,128)S(1)}, /*index=5*/s32[]{:T(128)}, s32[]{:T(128)}) while((s32[]{:T(128)}, f32[4,6,64,128]{3,2,1,0:T(8,128)}, s32[]{:T(128)}, f32[8,4,6,64,128]{4,3,2,1,0:T(8,128)}, ...), condition=%wide.region_8.9_spmd.clone, body=%wide.region_7.8_spmd.clone.sunk | while | flops 786436 | bytes 2359697 | solution.py:34
  286.2 6.5 add_convert_fusion
  295.7 48.9 %all_to_all.87 = bf16[4,512,384]{2,0,1:T(4,128)(2,1)S(1)} all-to-all(bf16[4,512,384]{2,0,1:T(4,128)(2,1)S(1)} %copy.422), channel_id=1, replica_groups=mesh['shard'=8,'head'=4] {'head'}, dimensions={1} | all-to-all | bytes 3145728 | tf_op jit(solution)/shard_map/all_to_all | solution.py:200
  351.4 5.5 multiply_reduce_fusion.5
  364.9 40.8 %all_to_all.88 = bf16[4,128,1536]{1,0,2:T(4,128)(2,1)S(1)} all-to-all(bf16[4,128,1536]{1,0,2:T(4,128)(2,1)} %reshape.1006), channel_id=1, replica_groups=mesh['shard'=8,'head'=4] {'head'}, dimensions={2} | all-to-all | bytes 3145728 | tf_op jit(solution)/shard_map/all_to_all | solution.py:229
  413.7 6.0 fusion.172
  424.6 38.8 %all-gather.17.cloned.1.call-done = f32[32,6,64,128]{3,2,1,0:T(8,128)} async-done(((f32[4,6,64,128]{3,2,1,0:T(8,128)}), f32[32,6,64,128]{3,2,1,0:T(8,128)}) %all-gather.17.cloned.1.call-update) | async-done | bytes 6291472 | tf_op jit(solution)/shard_map/all_gather | solution.py:21
  463.4 19.2 %while.214 = (s32[]{:T(128)}, f32[4,6,64,128]{3,2,1,0:T(8,128)}, s32[]{:T(128)}, f32[8,4,6,64,128]{4,3,2,1,0:T(8,128)}, f32[8,4,6]{2,1,0:T(4,128)S(1)}, /*index=5*/s32[]{:T(128)}, s32[]{:T(128)}, s32[]{:T(128)}, s32[]{:T(128)}) while((s32[]{:T(128)}, f32[4,6,64,128]{3,2,1,0:T(8,128)}, s32[]{:T(128)}, ...), condition=%wide.region_12.13_spmd.clone, body=%wide.region_11.12_spmd.clone.sunk | while | flops 786440 | bytes 2359759 | solution.py:34
  482.6 710.4 %while.211 = (s32[]{:T(128)}, f32[4,515,384]{2,0,1:T(4,128)}, f32[4,515,256]{2,0,1:T(4,128)}, bf16[4,512,6]{1,2,0:T(8,128)(2,1)}, f32[4,4,384]{2,1,0:T(4,128)}, ...) while((s32[]{:T(128)}, f32[4,515,384]{2,0,1:T(4,128)}, ...), condition=%wide.region_42.43_spmd, body=%wide.region_13.42_spmd.sunk | while | flops 1838452224 | bytes 153608192 | solution.py:282
  501.1 5.9 fusion.279
  507.2 27.8 %while.215 = (s32[]{:T(128)}, f32[6,64,128]{2,1,0:T(8,128)S(1)}, f32[2,256,256,6]{2,1,3,0:T(8,128)}, f32[2,128,256]{1,2,0:T(8,128)}, f32[2,256,256,1]{2,1,3,0:T(...) while((s32[]{:T(128)}, f32[6,64,128]{2,1,0:T(8,128)S(1)}, ...), condition=%wide.region_17.17_spmd.clone, body=%wide.region_14.16_spmd.clone.sunk | while | flops 404720640 | bytes 34438748 | solution.py:73
  543.7 66.3 %while.216 = (s32[]{:T(128)}, f32[6,64,128]{2,1,0:T(8,128)S(1)}, f32[2,256,6,64]{1,0,3,2:T(2,128)}, f32[2,256,128]{2,1,0:T(8,128)}, f32[2,256,128]{2,1,0:T(8,128...) while((s32[]{:T(128)}, f32[6,64,128]{2,1,0:T(8,128)S(1)}, ...), condition=%wide.region_28.28_spmd.clone, body=%wide.region_18.27_spmd.clone.sunk | while | flops 1414411776 | bytes 34215792 | solution.py:73
  560.0 7.6 reduce-window.71
  567.9 9.0 dynamic_update_slice.350
  593.2 7.6 reduce-window.71
  601.1 9.0 dynamic_update_slice.350
  628.9 12.6 dynamic_update_slice.328
  643.6 16.7 %dynamic_update_slice.327 = f32[4,515,384]{2,0,1:T(4,128)} dynamic-update-slice(f32[4,515,384]{2,0,1:T(4,128)} %get-tuple-element.3880, f32[1,515,384]{2,0,1:T(1,128)S(1)} %copy.663, s32[]{:T(128)S(6)} %copy.841, s32[]{:T(128)} %constant.407.clone.1..sunk, s32[]{:T(128)} %constant.407.clone.1..sunk) | dynamic-update-slice | bytes 1582084 | tf_op jit(solution)/shard_map/while/body/jit(dynamic_update_index_in_dim)/dynamic_update_slice | solution.py:282
  678.6 5.9 fusion.279
  684.6 27.8 %while.215 = (s32[]{:T(128)}, f32[6,64,128]{2,1,0:T(8,128)S(1)}, f32[2,256,256,6]{2,1,3,0:T(8,128)}, f32[2,128,256]{1,2,0:T(8,128)}, f32[2,256,256,1]{2,1,3,0:T(...) while((s32[]{:T(128)}, f32[6,64,128]{2,1,0:T(8,128)S(1)}, ...), condition=%wide.region_17.17_spmd.clone, body=%wide.region_14.16_spmd.clone.sunk | while | flops 404720640 | bytes 34438748 | solution.py:73
  721.1 66.3 %while.216 = (s32[]{:T(128)}, f32[6,64,128]{2,1,0:T(8,128)S(1)}, f32[2,256,6,64]{1,0,3,2:T(2,128)}, f32[2,256,128]{2,1,0:T(8,128)}, f32[2,256,128]{2,1,0:T(8,128...) while((s32[]{:T(128)}, f32[6,64,128]{2,1,0:T(8,128)S(1)}, ...), condition=%wide.region_28.28_spmd.clone, body=%wide.region_18.27_spmd.clone.sunk | while | flops 1414411776 | bytes 34215792 | solution.py:73
  737.4 7.6 reduce-window.71
  745.3 9.0 dynamic_update_slice.350
  770.6 7.6 reduce-window.71
  778.5 9.0 dynamic_update_slice.350
  806.3 12.6 dynamic_update_slice.328
  821.0 16.7 %dynamic_update_slice.327 = f32[4,515,384]{2,0,1:T(4,128)} dynamic-update-slice(f32[4,515,384]{2,0,1:T(4,128)} %get-tuple-element.3880, f32[1,515,384]{2,0,1:T(1,128)S(1)} %copy.663, s32[]{:T(128)S(6)} %copy.841, s32[]{:T(128)} %constant.407.clone.1..sunk, s32[]{:T(128)} %constant.407.clone.1..sunk) | dynamic-update-slice | bytes 1582084 | tf_op jit(solution)/shard_map/while/body/jit(dynamic_update_index_in_dim)/dynamic_update_slice | solution.py:282
  856.3 5.9 fusion.279
  862.3 27.8 %while.215 = (s32[]{:T(128)}, f32[6,64,128]{2,1,0:T(8,128)S(1)}, f32[2,256,256,6]{2,1,3,0:T(8,128)}, f32[2,128,256]{1,2,0:T(8,128)}, f32[2,256,256,1]{2,1,3,0:T(...) while((s32[]{:T(128)}, f32[6,64,128]{2,1,0:T(8,128)S(1)}, ...), condition=%wide.region_17.17_spmd.clone, body=%wide.region_14.16_spmd.clone.sunk | while | flops 404720640 | bytes 34438748 | solution.py:73
  898.7 66.3 %while.216 = (s32[]{:T(128)}, f32[6,64,128]{2,1,0:T(8,128)S(1)}, f32[2,256,6,64]{1,0,3,2:T(2,128)}, f32[2,256,128]{2,1,0:T(8,128)}, f32[2,256,128]{2,1,0:T(8,128...) while((s32[]{:T(128)}, f32[6,64,128]{2,1,0:T(8,128)S(1)}, ...), condition=%wide.region_28.28_spmd.clone, body=%wide.region_18.27_spmd.clone.sunk | while | flops 1414411776 | bytes 34215792 | solution.py:73
  915.1 7.6 reduce-window.71
  923.0 9.0 dynamic_update_slice.350
  948.2 7.6 reduce-window.71
  956.1 9.0 dynamic_update_slice.350
  984.0 12.6 dynamic_update_slice.328
  998.7 16.7 %dynamic_update_slice.327 = f32[4,515,384]{2,0,1:T(4,128)} dynamic-update-slice(f32[4,515,384]{2,0,1:T(4,128)} %get-tuple-element.3880, f32[1,515,384]{2,0,1:T(1,128)S(1)} %copy.663, s32[]{:T(128)S(6)} %copy.841, s32[]{:T(128)} %constant.407.clone.1..sunk, s32[]{:T(128)} %constant.407.clone.1..sunk) | dynamic-update-slice | bytes 1582084 | tf_op jit(solution)/shard_map/while/body/jit(dynamic_update_index_in_dim)/dynamic_update_slice | solution.py:282
  1033.5 5.9 fusion.279
  1039.4 27.8 %while.215 = (s32[]{:T(128)}, f32[6,64,128]{2,1,0:T(8,128)S(1)}, f32[2,256,256,6]{2,1,3,0:T(8,128)}, f32[2,128,256]{1,2,0:T(8,128)}, f32[2,256,256,1]{2,1,3,0:T(...) while((s32[]{:T(128)}, f32[6,64,128]{2,1,0:T(8,128)S(1)}, ...), condition=%wide.region_17.17_spmd.clone, body=%wide.region_14.16_spmd.clone.sunk | while | flops 404720640 | bytes 34438748 | solution.py:73
  1075.9 66.3 %while.216 = (s32[]{:T(128)}, f32[6,64,128]{2,1,0:T(8,128)S(1)}, f32[2,256,6,64]{1,0,3,2:T(2,128)}, f32[2,256,128]{2,1,0:T(8,128)}, f32[2,256,128]{2,1,0:T(8,128...) while((s32[]{:T(128)}, f32[6,64,128]{2,1,0:T(8,128)S(1)}, ...), condition=%wide.region_28.28_spmd.clone, body=%wide.region_18.27_spmd.clone.sunk | while | flops 1414411776 | bytes 34215792 | solution.py:73
  1092.2 7.6 reduce-window.71
  1100.1 9.0 dynamic_update_slice.350
  1125.4 7.6 reduce-window.71
  1133.3 9.0 dynamic_update_slice.350
  1161.1 12.6 dynamic_update_slice.328
  1175.8 16.7 %dynamic_update_slice.327 = f32[4,515,384]{2,0,1:T(4,128)} dynamic-update-slice(f32[4,515,384]{2,0,1:T(4,128)} %get-tuple-element.3880, f32[1,515,384]{2,0,1:T(1,128)S(1)} %copy.663, s32[]{:T(128)S(6)} %copy.841, s32[]{:T(128)} %constant.407.clone.1..sunk, s32[]{:T(128)} %constant.407.clone.1..sunk) | dynamic-update-slice | bytes 1582084 | tf_op jit(solution)/shard_map/while/body/jit(dynamic_update_index_in_dim)/dynamic_update_slice | solution.py:282
  1220.7 18.4 %all-to-all-done.5 = bf16[4,512,1,256]{3,0,2,1:T(4,128)(2,1)S(1)} async-done(((bf16[4,512,1,256]{3,0,2,1:T(4,128)(2,1)}), bf16[4,512,1,256]{3,0,2,1:T(4,128)(2,1)S(1)}, u32[]{:S(2)}, u32[]{:S(2)}) %all-to-all-start.5) | async-done | bytes 1048608 | tf_op jit(solution)/shard_map/all_to_all | solution.py:296
  1244.9 34.3 %all-to-all-done.4 = bf16[4,512,384]{2,0,1:T(4,128)(2,1)S(1)} async-done(((bf16[4,512,384]{2,0,1:T(4,128)(2,1)}), bf16[4,512,384]{2,0,1:T(4,128)(2,1)S(1)}, u32[]{:S(2)}, u32[]{:S(2)}) %all-to-all-start.4) | async-done | bytes 1572896 | tf_op jit(solution)/shard_map/all_to_all | solution.py:299
  1282.8 11.3 fusion.193
  1302.0 7.4 fusion.186
  1309.4 38.4 %all-reduce.20 = (f32[768]{0:T(1024)}, f32[4,1792]{1,0:T(4,128)}, f32[1792]{0:T(1024)}, f32[24]{0:T(128)}, f32[24]{0:T(128)}, /*index=5*/f32[24]{0:T(128)}, f32[1536]{0:T(1024)}) all-reduce(f32[768]{0:T(1024)S(1)} %get-tuple-element.2456, ...), channel_id=1, replica_groups=mesh['shard'=8,'head'=4] {'shard','head'}, use_global_device_ids=true, to_apply=%region_46.47 | all-reduce | flops 11336 | bytes 90688 | tf_op jit(solution)/shard_map/psum | solution.py:351
  1349.5 85.2 %reduce-scatter.7.cloned.1.call-done = f32[24,3352]{1,0:T(8,128)} async-done(((f32[768,3352]{1,0:T(8,128)}), f32[24,3352]{1,0:T(8,128)}) %reduce-scatter.7.cloned.1.call-update) | async-done | bytes 321808
  (1498 shorter events, 621.8 us)
Async XLA Ops:
  7.2 72.0 %all-gather.9.cloned.1.call-start = ((), (), s32[]{:S(2)}) async-start(), calls=%async_computation.9 | async-start | bytes 5474304 | tf_op jit(solution)/shard_map/all_gather | solution.py:134
  7.9 119.8 %all-gather.11.cloned.1.call-start = ((), (), s32[]{:S(2)}) async-start(), calls=%async_computation.10 | async-start | bytes 1310720 | tf_op jit(solution)/shard_map/all_gather | solution.py:161
  84.8 11.5 copy-start.23
  88.2 9.0 all-to-all-start
  97.2 50.9 %all-to-all-start.1 = ((bf16[4,128,1536]{1,0,2:T(4,128)(2,1)}), bf16[4,128,1536]{1,0,2:T(4,128)(2,1)S(1)}, u32[]{:S(2)}, u32[]{:S(2)}) async-start(bf16[4,128,1536]{1,0,2:T(4,128)(2,1)} %reshape.994), calls=%async_computation.1 | async-start | bytes 3145728 | tf_op jit(solution)/shard_map/all_to_all | solution.py:158
  101.4 165.5 %all-gather.15.cloned.1.call-start = ((), (), s32[]{:S(2)}) async-start(), calls=%async_computation.13 | async-start | bytes 7077888 | tf_op jit(solution)/shard_map/all_gather | solution.py:21
  128.5 2.1 collective-permute-start.1
  153.1 3.7 collective-permute-start
  169.1 48.9 %copy-start.74 = (f32[24]{0:T(128)S(1)}, f32[24]{0:T(128)}, u32[]{:S(2)}) copy-start(f32[24]{0:T(128)} %param.34) | copy-start | bytes 292
  217.3 134.1 %all-gather.13.cloned.1.call-start = ((), (), s32[]{:S(2)}) async-start(), calls=%async_computation.11 | async-start | bytes 2433024 | tf_op jit(solution)/shard_map/all_gather | solution.py:135
  217.9 245.5 %all-gather.17.cloned.1.call-start = ((), (), s32[]{:S(2)}) async-start(), calls=%async_computation.14 | async-start | bytes 7077888 | tf_op jit(solution)/shard_map/all_gather | solution.py:21
  242.3 43.9 %copy-start.14 = (f32[4,512,384]{1,2,0:T(8,128)S(1)}, f32[4,512,384]{1,2,0:T(8,128)}, u32[]{:S(2)}) copy-start(f32[4,512,384]{1,2,0:T(8,128)} %divide_multiply_fusion) | copy-start | bytes 9437188
  351.3 68.5 %copy-start.11 = (f32[512,1536]{0,1:T(8,128)}, f32[512,1536]{0,1:T(8,128)S(1)}, u32[]{:S(2)}) copy-start(f32[512,1536]{0,1:T(8,128)S(1)} %get-tuple-element.2670) | copy-start | bytes 9437188
  351.4 68.5 %copy-start.55 = (f32[512]{0:T(512)}, f32[512]{0:T(512)S(1)}, u32[]{:S(2)}) copy-start(f32[512]{0:T(512)S(1)} %get-tuple-element.2725) | copy-start | bytes 6148
  419.7 929.8 %reduce-scatter.5.cloned.1.call-start = ((), (), s32[]{:S(2)}) async-start(), calls=%async_computation.12 | async-start | bytes 4866048 | tf_op jit(solution)/shard_map/reduce_scatter | solution.py:349
  463.4 19.2 %slice-start = ((f32[4,1792]{1,0:T(4,128)}), f32[4,256]{1,0:T(4,128)S(1)}, s32[]{:S(2)}) async-start(f32[4,1792]{1,0:T(4,128)} %param.30), calls=%async_computation.16 | async-start | bytes 8192 | tf_op jit(solution)/shard_map/slice | solution.py:168
  493.7 13.3 copy-start.7
  493.7 13.4 copy-start.8
  493.8 41.3 %copy-start.5 = (f32[1,512,384]{1,2,0:T(8,128)}, f32[1,512,384]{1,2,0:T(8,128)S(1)}, u32[]{:S(2)}) copy-start(f32[1,512,384]{1,2,0:T(8,128)S(1)} %get-tuple-element.3430) | copy-start | bytes 2359300 | tf_op jit(solution)/shard_map/while
  641.8 18.5 %copy-start.32 = (f32[4,512,6]{1,0,2:T(4,128)S(1)}, f32[4,512,6]{1,0,2:T(4,128)}, u32[]{:S(2)}) copy-start(f32[4,512,6]{1,0,2:T(4,128)} %copy-done.31) | copy-start | bytes 147460 | tf_op jit(solution)/shard_map/while
  641.8 18.5 %copy-start.40 = (f32[4,384]{1,0:T(4,128)S(1)}, f32[4,384]{1,0:T(4,128)}, u32[]{:S(2)}) copy-start(f32[4,384]{1,0:T(4,128)} %copy-done.39) | copy-start | bytes 18436 | tf_op jit(solution)/shard_map/while
  641.8 18.5 %copy-start.43 = (f32[1,6]{1,0:T(1,128)S(1)}, f32[1,6]{1,0:T(1,128)}, u32[]{:S(2)}) copy-start(f32[1,6]{1,0:T(1,128)} %copy-done.42) | copy-start | bytes 76 | tf_op jit(solution)/shard_map/while
  641.8 18.5 %copy-start.45 = (f32[6]{0:T(128)S(1)}, f32[6]{0:T(128)}, u32[]{:S(2)}) copy-start(f32[6]{0:T(128)} %copy-done.44) | copy-start | bytes 76 | tf_op jit(solution)/shard_map/while
  641.9 18.5 %copy-start.48 = (f32[4,256]{1,0:T(4,128)S(1)}, f32[4,256]{1,0:T(4,128)}, u32[]{:S(2)}) copy-start(f32[4,256]{1,0:T(4,128)} %copy-done.47) | copy-start | bytes 12292 | tf_op jit(solution)/shard_map/while
  641.9 18.5 %copy-start.52 = (f32[6]{0:T(128)S(1)}, f32[6]{0:T(128)}, u32[]{:S(2)}) copy-start(f32[6]{0:T(128)} %copy-done.51) | copy-start | bytes 76 | tf_op jit(solution)/shard_map/while
  641.9 18.5 %copy-start.54 = (f32[256]{0:T(256)S(1)}, f32[256]{0:T(256)}, u32[]{:S(2)}) copy-start(f32[256]{0:T(256)} %copy-done.53) | copy-start | bytes 3076 | tf_op jit(solution)/shard_map/while
  671.3 13.2 copy-start.7
  671.3 13.3 copy-start.8
  671.3 41.2 %copy-start.5 = (f32[1,512,384]{1,2,0:T(8,128)}, f32[1,512,384]{1,2,0:T(8,128)S(1)}, u32[]{:S(2)}) copy-start(f32[1,512,384]{1,2,0:T(8,128)S(1)} %get-tuple-element.3430) | copy-start | bytes 2359300 | tf_op jit(solution)/shard_map/while
  819.2 18.5 %copy-start.32 = (f32[4,512,6]{1,0,2:T(4,128)S(1)}, f32[4,512,6]{1,0,2:T(4,128)}, u32[]{:S(2)}) copy-start(f32[4,512,6]{1,0,2:T(4,128)} %copy-done.31) | copy-start | bytes 147460 | tf_op jit(solution)/shard_map/while
  819.2 18.5 %copy-start.40 = (f32[4,384]{1,0:T(4,128)S(1)}, f32[4,384]{1,0:T(4,128)}, u32[]{:S(2)}) copy-start(f32[4,384]{1,0:T(4,128)} %copy-done.39) | copy-start | bytes 18436 | tf_op jit(solution)/shard_map/while
  819.2 18.5 %copy-start.43 = (f32[1,6]{1,0:T(1,128)S(1)}, f32[1,6]{1,0:T(1,128)}, u32[]{:S(2)}) copy-start(f32[1,6]{1,0:T(1,128)} %copy-done.42) | copy-start | bytes 76 | tf_op jit(solution)/shard_map/while
  819.2 18.5 %copy-start.45 = (f32[6]{0:T(128)S(1)}, f32[6]{0:T(128)}, u32[]{:S(2)}) copy-start(f32[6]{0:T(128)} %copy-done.44) | copy-start | bytes 76 | tf_op jit(solution)/shard_map/while
  819.2 18.5 %copy-start.48 = (f32[4,256]{1,0:T(4,128)S(1)}, f32[4,256]{1,0:T(4,128)}, u32[]{:S(2)}) copy-start(f32[4,256]{1,0:T(4,128)} %copy-done.47) | copy-start | bytes 12292 | tf_op jit(solution)/shard_map/while
  819.3 18.5 %copy-start.52 = (f32[6]{0:T(128)S(1)}, f32[6]{0:T(128)}, u32[]{:S(2)}) copy-start(f32[6]{0:T(128)} %copy-done.51) | copy-start | bytes 76 | tf_op jit(solution)/shard_map/while
  819.3 18.5 %copy-start.54 = (f32[256]{0:T(256)S(1)}, f32[256]{0:T(256)}, u32[]{:S(2)}) copy-start(f32[256]{0:T(256)} %copy-done.53) | copy-start | bytes 3076 | tf_op jit(solution)/shard_map/while
  849.0 13.2 copy-start.7
  849.0 13.3 copy-start.8
  849.0 41.1 %copy-start.5 = (f32[1,512,384]{1,2,0:T(8,128)}, f32[1,512,384]{1,2,0:T(8,128)S(1)}, u32[]{:S(2)}) copy-start(f32[1,512,384]{1,2,0:T(8,128)S(1)} %get-tuple-element.3430) | copy-start | bytes 2359300 | tf_op jit(solution)/shard_map/while
  996.9 18.5 %copy-start.32 = (f32[4,512,6]{1,0,2:T(4,128)S(1)}, f32[4,512,6]{1,0,2:T(4,128)}, u32[]{:S(2)}) copy-start(f32[4,512,6]{1,0,2:T(4,128)} %copy-done.31) | copy-start | bytes 147460 | tf_op jit(solution)/shard_map/while
  996.9 18.5 %copy-start.40 = (f32[4,384]{1,0:T(4,128)S(1)}, f32[4,384]{1,0:T(4,128)}, u32[]{:S(2)}) copy-start(f32[4,384]{1,0:T(4,128)} %copy-done.39) | copy-start | bytes 18436 | tf_op jit(solution)/shard_map/while
  996.9 18.5 %copy-start.43 = (f32[1,6]{1,0:T(1,128)S(1)}, f32[1,6]{1,0:T(1,128)}, u32[]{:S(2)}) copy-start(f32[1,6]{1,0:T(1,128)} %copy-done.42) | copy-start | bytes 76 | tf_op jit(solution)/shard_map/while
  996.9 18.5 %copy-start.45 = (f32[6]{0:T(128)S(1)}, f32[6]{0:T(128)}, u32[]{:S(2)}) copy-start(f32[6]{0:T(128)} %copy-done.44) | copy-start | bytes 76 | tf_op jit(solution)/shard_map/while
  996.9 18.5 %copy-start.48 = (f32[4,256]{1,0:T(4,128)S(1)}, f32[4,256]{1,0:T(4,128)}, u32[]{:S(2)}) copy-start(f32[4,256]{1,0:T(4,128)} %copy-done.47) | copy-start | bytes 12292 | tf_op jit(solution)/shard_map/while
  996.9 18.5 %copy-start.52 = (f32[6]{0:T(128)S(1)}, f32[6]{0:T(128)}, u32[]{:S(2)}) copy-start(f32[6]{0:T(128)} %copy-done.51) | copy-start | bytes 76 | tf_op jit(solution)/shard_map/while
  996.9 18.5 %copy-start.54 = (f32[256]{0:T(256)S(1)}, f32[256]{0:T(256)}, u32[]{:S(2)}) copy-start(f32[256]{0:T(256)} %copy-done.53) | copy-start | bytes 3076 | tf_op jit(solution)/shard_map/while
  1026.1 13.2 copy-start.7
  1026.1 13.3 copy-start.8
  1026.1 41.1 %copy-start.5 = (f32[1,512,384]{1,2,0:T(8,128)}, f32[1,512,384]{1,2,0:T(8,128)S(1)}, u32[]{:S(2)}) copy-start(f32[1,512,384]{1,2,0:T(8,128)S(1)} %get-tuple-element.3430) | copy-start | bytes 2359300 | tf_op jit(solution)/shard_map/while
  1174.0 18.5 %copy-start.32 = (f32[4,512,6]{1,0,2:T(4,128)S(1)}, f32[4,512,6]{1,0,2:T(4,128)}, u32[]{:S(2)}) copy-start(f32[4,512,6]{1,0,2:T(4,128)} %copy-done.31) | copy-start | bytes 147460 | tf_op jit(solution)/shard_map/while
  1174.0 18.5 %copy-start.40 = (f32[4,384]{1,0:T(4,128)S(1)}, f32[4,384]{1,0:T(4,128)}, u32[]{:S(2)}) copy-start(f32[4,384]{1,0:T(4,128)} %copy-done.39) | copy-start | bytes 18436 | tf_op jit(solution)/shard_map/while
  1174.0 18.5 %copy-start.43 = (f32[1,6]{1,0:T(1,128)S(1)}, f32[1,6]{1,0:T(1,128)}, u32[]{:S(2)}) copy-start(f32[1,6]{1,0:T(1,128)} %copy-done.42) | copy-start | bytes 76 | tf_op jit(solution)/shard_map/while
  1174.1 18.5 %copy-start.45 = (f32[6]{0:T(128)S(1)}, f32[6]{0:T(128)}, u32[]{:S(2)}) copy-start(f32[6]{0:T(128)} %copy-done.44) | copy-start | bytes 76 | tf_op jit(solution)/shard_map/while
  1174.1 18.5 %copy-start.48 = (f32[4,256]{1,0:T(4,128)S(1)}, f32[4,256]{1,0:T(4,128)}, u32[]{:S(2)}) copy-start(f32[4,256]{1,0:T(4,128)} %copy-done.47) | copy-start | bytes 12292 | tf_op jit(solution)/shard_map/while
  1174.1 18.5 %copy-start.52 = (f32[6]{0:T(128)S(1)}, f32[6]{0:T(128)}, u32[]{:S(2)}) copy-start(f32[6]{0:T(128)} %copy-done.51) | copy-start | bytes 76 | tf_op jit(solution)/shard_map/while
  1174.1 18.5 %copy-start.54 = (f32[256]{0:T(256)S(1)}, f32[256]{0:T(256)}, u32[]{:S(2)}) copy-start(f32[256]{0:T(256)} %copy-done.53) | copy-start | bytes 3076 | tf_op jit(solution)/shard_map/while
  1193.7 10.4 collective-permute-start.3
  1199.4 10.4 all-to-all-start.6
  1209.8 29.3 %all-to-all-start.5 = ((bf16[4,512,1,256]{3,0,2,1:T(4,128)(2,1)}), bf16[4,512,1,256]{3,0,2,1:T(4,128)(2,1)S(1)}, u32[]{:S(2)}, u32[]{:S(2)}) async-start(bf16[4,512,1,256]{3,0,2,1:T(4,128)(2,1)} %bitcast.83), calls=%async_computation.5 | async-start | bytes 2097152 | tf_op jit(solution)/shard_map/all_to_all | solution.py:296
  1214.0 3.7 collective-permute-start.2
  1239.1 40.1 %all-to-all-start.4 = ((bf16[4,512,384]{2,0,1:T(4,128)(2,1)}), bf16[4,512,384]{2,0,1:T(4,128)(2,1)S(1)}, u32[]{:S(2)}, u32[]{:S(2)}) async-start(bf16[4,512,384]{2,0,1:T(4,128)(2,1)} %pad_maximum_fusion.1), calls=%async_computation.4 | async-start | bytes 3145728 | tf_op jit(solution)/shard_map/all_to_all | solution.py:299
  1242.7 192.0 %reduce-scatter.7.cloned.1.call-start = ((), (), s32[]{:S(2)}) async-start(), calls=%async_computation.15 | async-start | bytes 10948608
  1301.9 45.9 %copy-start.24 = (bf16[4,128,768]{2,1,0:T(8,128)(2,1)S(1)}, bf16[4,128,768]{2,1,0:T(8,128)(2,1)}, u32[]{:S(2)}) copy-start(bf16[4,128,768]{2,1,0:T(8,128)(2,1)} %param.27) | copy-start | bytes 2359300
  1301.9 45.9 %copy-start.25 = (bf16[4,128,768]{2,1,0:T(8,128)(2,1)S(1)}, bf16[4,128,768]{2,1,0:T(8,128)(2,1)}, u32[]{:S(2)}) copy-start(bf16[4,128,768]{2,1,0:T(8,128)(2,1)} %param.37) | copy-start | bytes 2359300
  (170 other events, 974.4 us)
Sparse Core Ops, SparseCore 0:
  10.8 68.3 all-gather.8
  87.7 39.9 all-gather.10
  217.4 49.4 all-gather.14
  269.6 62.5 all-gather.12
  419.8 43.5 all-gather.16
  469.3 107.3 reduce-scatter.4
  1294.3 140.2 reduce-scatter.6
where the time goes:
time: 1460 us; the launch traced here: 1440 us
  local copies, waits for them, and re-layouts  453 us (31%)
  other arithmetic  308 us (21%)
  waiting for transfers between devices  306 us (21%)
  matrix products  185 us (13%)
  blocking collectives  143 us (10%)
  starting transfers between devices  25.2 us (2%)
  between operations  15.1 us (1%)
    dynamic_update_slice x36, local copies, waits for them, and re-layouts, shards(): lax.map(local_backward, (padded_x, padded_bc, dt_in, entering, mixed_back...  148 us
    dynamic_update_slice x120, local copies, waits for them, and re-layouts, block_scan(): final_state, outputs = lax.scan(advance, initial, blocks)  104 us
    another operation x111, other arithmetic  101 us
    unnamed x8, waiting for transfers between devices  86.5 us
    all_gather x1, waiting for transfers between devices, shards(): lax.all_gather(w_in, ('shard', 'head'), axis=0, tiled=True)  66.5 us
    all_gather x2, waiting for transfers between devices, entering_2(): everything = jax.tree.map(lambda part: lax.all_gather(part, axis), array)  59.3 us
    dot_general x18, matrix products, advance(): inside = jnp.einsum('tsh,shp->thp', mixing, x_block, precision=HIGHEST)  56.1 us
    all_to_all x1, blocking collectives, shards(): lax.all_to_all(mixed, 'head', split_axis=1, concat_axis=2, tiled=True)  48.9 us
  transfers between devices with their start and end apart: 16, of which 11 were waited for; matrix products, arithmetic and copies ran while one was open for 57% of the time, Pallas kernels for 0%

commit v1 on v0

v1 whole, which is shorter than its diff:
```python
import functools

import jax
import jax.numpy as jnp
from jax import lax
from jax.experimental import pallas as pl
from jax.experimental.pallas import tpu as pltpu
from jax.sharding import PartitionSpec as P

F32, BF16 = jnp.float32, jnp.bfloat16
EPSILON = 1e-05
HIGHEST = lax.Precision.HIGHEST
CHUNK = 128
HALO = 16
LANES = 128
VMEM_LIMIT = 60 * 1024 * 1024


def dot(a, b, contract=((1,), (0,)), precision=None):
    return lax.dot_general(a, b, (contract, ((), ())), precision=precision, preferred_element_type=F32)


ROWS = ((0,), (0,))
LAST = ((1,), (1,))


def tile_of(rows, most):
    return max(t for t in range(16, most + 1, 16) if rows % t == 0)


def fill_spread(e_ref, head_dim, heads):
    channels = e_ref.shape[1]
    row = lax.broadcasted_iota(jnp.int32, (LANES, channels), 0)
    col = lax.broadcasted_iota(jnp.int32, (LANES, channels), 1)
    one = jnp.where((col >= row * head_dim) & (col < (row + 1) * head_dim), 1.0, 0.0).astype(BF16)
    e_ref[0:LANES, :] = one
    e_ref[LANES : 2 * LANES, :] = one


def halves(value):
    high = value.astype(BF16)
    return high, (value - high.astype(F32)).astype(BF16)


def spread(value, e_ref):
    return dot(jnp.concatenate(halves(value), axis=1), e_ref[...])


def head_sums(value, e_ref):
    high, low = halves(value)
    e = e_ref[0:LANES, :]
    return dot(high, e, LAST) + dot(low, e, LAST)


def split_pair(pair):
    lane = lax.broadcasted_iota(jnp.int32, pair.shape, 1)
    zero = jnp.zeros_like(pair)
    half = pair.shape[1] // 2
    return jnp.concatenate([jnp.where(lane < half, pair, zero), jnp.where(lane >= half, pair, zero)], axis=0)


def silu_slope(values, logistic):
    return logistic * (1.0 + values * (1.0 - logistic))


def softplus(v):
    return jnp.maximum(v, 0.0) + jnp.log1p(jnp.exp(-jnp.abs(v)))


def conv_pre(raw_ref, w_ref, b_ref, r0, rows, c0, cols):
    taps = w_ref.shape[0]
    window = raw_ref[pl.ds(r0, rows + HALO), pl.ds(c0, cols)].astype(F32)
    total = jnp.broadcast_to(b_ref[:, pl.ds(c0, cols)], (rows, cols))
    shifts = []
    for k in range(taps):
        start = HALO - taps + 1 + k
        shifts.append(window[start : start + rows])
        total = total + w_ref[k : k + 1, pl.ds(c0, cols)] * shifts[-1]
    return total, shifts


def project_kernel(tok, w_in, gain, conv_w, conv_b, dt_bias, a_log,
                   normed, gate, raw, dt_raw, act, dt, cum, cum_t, loc, dec, e, state):
    ext, d = tok.shape
    inner = gate.shape[1]
    conv_ch = raw.shape[1]
    proj = w_in.shape[1]
    heads = proj - inner - conv_ch
    state_n = (conv_ch - inner) // 2
    length = ext - HALO
    chunks = length // CHUNK
    fill_spread(e, inner // heads, heads)
    dt_raw[...] = jnp.zeros_like(dt_raw)
    rt = tile_of(ext, 192)
    ct = 512

    def norm_rows(i, _):
        rows = pl.ds(pl.multiple_of(i * 16, 16), 16)
        t = tok[rows, :].astype(F32)
        r = lax.rsqrt(jnp.mean(t * t, axis=-1, keepdims=True) + EPSILON)
        normed[rows, :] = (t * r * gain[...]).astype(BF16)
        return 0

    lax.fori_loop(0, ext // 16, norm_rows, 0)

    def proj_rows(i, _):
        rows = pl.ds(pl.multiple_of(i * rt, 16), rt)
        n = normed[rows, :]

        def gate_cols(j, _):
            cols = pl.ds(pl.multiple_of(j * ct, ct), ct)
            gate[rows, cols] = dot(n, w_in[:, cols]).astype(BF16)
            return 0

        def x_cols(j, _):
            cols = pl.ds(pl.multiple_of(j * ct, ct), ct)
            src = pl.ds(pl.multiple_of(inner + j * ct, ct), ct)
            raw[rows, cols] = dot(n, w_in[:, src]).astype(BF16)
            return 0

        lax.fori_loop(0, inner // ct, gate_cols, 0)
        lax.fori_loop(0, inner // ct, x_cols, 0)
        last = dot(n, w_in[:, 2 * inner :])
        raw[rows, inner:] = last[:, : conv_ch - inner].astype(BF16)
        dt_raw[rows, 0:heads] = last[:, conv_ch - inner :].astype(BF16).astype(F32)
        return 0

    lax.fori_loop(0, ext // rt, proj_rows, 0)

    def conv_tile(i, _):
        r0 = pl.multiple_of(i * 64, 64)

        def conv_cols(j, _):
            c0 = pl.multiple_of(j * 256, 256)
            pre, _s = conv_pre(raw, conv_w, conv_b, r0, 64, c0, 256)
            act[pl.ds(r0, 64), pl.ds(c0, 256)] = (pre * jax.nn.sigmoid(pre)).astype(BF16)
            return 0

        return lax.fori_loop(0, conv_ch // 256, conv_cols, 0)

    lax.fori_loop(0, length // 64, conv_tile, 0)

    t_i = lax.broadcasted_iota(jnp.int32, (CHUNK, CHUNK), 0)
    s_i = lax.broadcasted_iota(jnp.int32, (CHUNK, CHUNK), 1)
    tril = jnp.where(t_i >= s_i, 1.0, 0.0)
    rate = -jnp.exp(a_log[...])
    state[...] = jnp.zeros_like(state)
    dec[...] = jnp.zeros_like(dec)

    def chunk(c, _):
        rows = pl.ds(pl.multiple_of(c * CHUNK, CHUNK), CHUNK)
        step = softplus(dt_raw[pl.ds(pl.multiple_of(c * CHUNK + HALO, 16), CHUNK), :] + dt_bias[...])
        dt[rows, :] = step
        running = dot(tril, step * rate, precision=HIGHEST)
        cum[rows, :] = running
        cum_t[c] = running.T
        last = running[CHUNK - 1 : CHUNK, :]
        loc[c] = state[...]
        weight = jnp.exp(last - running) * step
        xw = (act[rows, 0:inner].astype(F32) * spread(weight, e)).astype(BF16)
        b = act[rows, inner : inner + state_n]
        kept = spread(jnp.exp(jnp.broadcast_to(last, (8, LANES))), e)[0:1]
        state[...] = state[...] * kept + dot(b, xw, ROWS)
        dec[...] = dec[...] + last
        return 0

    lax.fori_loop(0, chunks, chunk, 0)
    loc[chunks] = state[...]


def mix_kernel(tok, og, w_out, gate, act, dt, cum, cum_t, loc, enter, gain, skip,
               out, dy, dgate, gw_out, gain_grad, skip_grad, y_dot, states, direct, leave, e, y, xd, gn, dg, acc):
    length, inner = gate.shape[0] - HALO, gate.shape[1]
    state_n = loc.shape[1]
    chunks = length // CHUNK
    pairs = inner // LANES
    fill_spread(e, skip.shape[1] // 1, 0) if False else None
    head_dim = LANES // 2
    fill_spread(e, head_dim, 0)
    t_i = lax.broadcasted_iota(jnp.int32, (CHUNK, CHUNK), 0)
    s_i = lax.broadcasted_iota(jnp.int32, (CHUNK, CHUNK), 1)
    causal = t_i >= s_i
    acc[...] = jnp.zeros_like(acc)
    skip_grad[...] = jnp.zeros_like(skip_grad)
    states[0] = enter[...]

    def chunk(c, carried):
        rows = pl.ds(pl.multiple_of(c * CHUNK, CHUNK), CHUNK)
        running = cum[rows, :]
        step = dt[rows, :]
        last = running[CHUNK - 1 : CHUNK, :]
        grown = spread(jnp.exp(running), e)
        bb = act[rows, inner : inner + state_n]
        cc = act[rows, inner + state_n :]
        scores = dot(cc, bb, LAST)
        s_in = states[c].astype(BF16)
        y[...] = dot(cc, s_in) * grown
        xd[...] = (act[rows, 0:inner].astype(F32) * spread(step, e)).astype(BF16)
        for p in range(pairs):
            cols = slice(p * LANES, (p + 1) * LANES)
            mix = []
            for h in (2 * p, 2 * p + 1):
                gap = running[:, h : h + 1] - cum_t[c, h : h + 1, :]
                mix.append((scores * jnp.exp(jnp.where(causal, gap, -1e30))).astype(BF16))
            y[:, cols] = y[:, cols] + dot(jnp.concatenate(mix, axis=1), split_pair(xd[:, cols]))
        dg[...] = dot(og[rows, :], w_out[...], LAST)

        def rows16(i, _):
            sub = pl.ds(pl.multiple_of(i * 16, 16), 16)
            at = pl.ds(pl.multiple_of(c * CHUNK + i * 16, 16), 16)
            gate_f = gate[pl.ds(pl.multiple_of(c * CHUNK + i * 16 + HALO, 16), 16), :].astype(F32)
            x = act[at, 0:inner].astype(F32)
            mixed = (y[sub, :] + skip[...] * x).astype(BF16).astype(F32)
            logistic = jax.nn.sigmoid(gate_f)
            silu = gate_f * logistic
            gated = mixed * silu
            rms = lax.rsqrt(jnp.mean(gated * gated, axis=-1, keepdims=True) + EPSILON)
            unit = gated * rms
            gn[at, :] = (unit * gain[...]).astype(BF16)
            d_norm = dg[sub, :]
            both = d_norm * unit
            acc[...] = acc[...] + both[0:8] + both[8:16]
            scaled = d_norm * gain[...]
            d_gated = rms * (scaled - unit * jnp.mean(unit * scaled, axis=-1, keepdims=True))
            dy[at, :] = (d_gated * silu).astype(BF16)
            dgate[at, :] = (d_gated * mixed * silu_slope(gate_f, logistic)).astype(BF16)
            return 0

        lax.fori_loop(0, CHUNK // 16, rows16, 0)
        tok_f = tok[pl.ds(pl.multiple_of(c * CHUNK + HALO, 16), CHUNK), :].astype(F32)
        out[rows, :] = (tok_f + dot(gn[rows, :], w_out[...])).astype(BF16)
        dy_f = dy[rows, :].astype(F32)
        direct[c] = dot(cc, (dy_f * grown).astype(BF16), ROWS)
        y_dot[rows, :] = head_sums(dy_f * y[...], e)
        x_sum = head_sums(dy_f * act[rows, 0:inner].astype(F32), e)
        skip_grad[...] = skip_grad[...] + jnp.sum(x_sum, axis=0, keepdims=True)
        total = carried + last
        far = spread(jnp.exp(jnp.broadcast_to(total, (8, LANES))), e)[0:1]
        states[c + 1] = loc[c + 1] + enter[...] * far
        return total

    lax.fori_loop(0, chunks, chunk, jnp.zeros((1, LANES), F32))
    gain_grad[...] = jnp.sum(acc[...], axis=0, keepdims=True)

    leave[...] = jnp.zeros_like(leave)

    def back(i, _):
        c = chunks - 1 - i
        last = cum[pl.ds(pl.multiple_of(c * CHUNK + CHUNK - 8, 8), 8), :]
        leave[...] = leave[...] * spread(jnp.exp(last), e)[7:8] + direct[c]
        return 0

    lax.fori_loop(0, chunks, back, 0)

    def w_rows(i, _):
        cols = pl.ds(pl.multiple_of(i * 256, 256), 256)
        gw_out[cols, :] = dot(gn[:, cols], og[...], ROWS)
        return 0

    lax.fori_loop(0, inner // 256, w_rows, 0)


def back_kernel(raw, dt_raw, act, dt, cum, cum_t, dy, states, direct, leaving, y_dot, conv_w, conv_b, dt_bias, a_log, skip,
                d_pre, d_dt, w_grad, b_grad, bias_grad, rate_grad, e, xd, dxd, d_act, d_state, w_acc):
    length, inner = dy.shape
    conv_ch = raw.shape[1]
    state_n = states.shape[1]
    chunks = length // CHUNK
    pairs = inner // LANES
    fill_spread(e, LANES // 2, 0)
    s_i = lax.broadcasted_iota(jnp.int32, (CHUNK, CHUNK), 0)
    t_i = lax.broadcasted_iota(jnp.int32, (CHUNK, CHUNK), 1)
    causal = t_i >= s_i
    triu = jnp.where(causal, 1.0, 0.0)
    rate = -jnp.exp(a_log[...])
    w_acc[...] = jnp.zeros_like(w_acc)
    bias_grad[...] = jnp.zeros_like(bias_grad)
    rate_grad[...] = jnp.zeros_like(rate_grad)
    d_state[...] = leaving[...]
    d_pre[length:, :] = jnp.zeros((HALO, conv_ch), BF16)

    def chunk(i, _):
        c = chunks - 1 - i
        rows = pl.ds(pl.multiple_of(c * CHUNK, CHUNK), CHUNK)
        running = cum[rows, :]
        step = dt[rows, :]
        last = running[CHUNK - 1 : CHUNK, :]
        ds = d_state[...]
        dsb = ds.astype(BF16)
        bb = act[rows, inner : inner + state_n]
        cc = act[rows, inner + state_n :]
        scores = dot(bb, cc, LAST)
        tail = spread(jnp.exp(last - running), e)
        dxd[...] = dot(bb, dsb) * tail
        x_f = act[rows, 0:inner].astype(F32)
        xd_f = x_f * spread(step, e)
        xd[...] = xd_f.astype(BF16)
        d_scores = jnp.zeros((CHUNK, CHUNK), F32)
        for p in range(pairs):
            cols = slice(p * LANES, (p + 1) * LANES)
            dyp = dy[rows, cols]
            d_mix = dot(split_pair(xd[:, cols]), dyp, LAST)
            mix = []
            for k in range(2):
                h = 2 * p + k
                gap = cum_t[c, h : h + 1, :] - running[:, h : h + 1]
                decay = jnp.exp(jnp.where(causal, gap, -1e30))
                mix.append((scores * decay).astype(BF16))
                d_scores = d_scores + decay * d_mix[k * CHUNK : (k + 1) * CHUNK]
            dxd[:, cols] = dxd[:, cols] + dot(jnp.concatenate(mix, axis=1), split_pair(dyp))
        dsc = d_scores.astype(BF16)
        dy_f = dy[rows, :].astype(F32)
        d_act[:, inner : inner + state_n] = dot(dsc, cc) + dot((xd_f * tail).astype(BF16), dsb, LAST)
        grown = spread(jnp.exp(running), e)
        d_act[:, inner + state_n :] = dot(dsc, bb, ROWS) + dot((dy_f * grown).astype(BF16), states[c].astype(BF16), LAST)
        dxd_f = dxd[...]
        d_act[:, 0:inner] = skip[...] * dy_f + spread(step, e) * dxd_f
        d_step = head_sums(x_f * dxd_f, e)
        base = head_sums(jnp.broadcast_to(jnp.sum(ds * states[c + 1], axis=0, keepdims=True), (8, inner)), e)[0:1]
        d_log = dot(triu, y_dot[rows, :] - step * d_step, precision=HIGHEST) + base
        rate_grad[...] = rate_grad[...] + jnp.sum(d_log * step, axis=0, keepdims=True) * rate
        logistic = jax.nn.sigmoid(dt_raw[pl.ds(pl.multiple_of(c * CHUNK + HALO, 16), CHUNK), :] + dt_bias[...])
        d_raw = (d_step + d_log * rate) * logistic
        d_dt[rows, :] = d_raw
        bias_grad[...] = bias_grad[...] + jnp.sum(d_raw, axis=0, keepdims=True)
        kept = spread(jnp.exp(jnp.broadcast_to(last, (8, LANES))), e)[0:1]
        d_state[...] = ds * kept + direct[c]

        def conv_tile(i, _):
            r0 = pl.multiple_of(c * CHUNK + i * 64, 64)

            def conv_cols(j, _):
                c0 = pl.multiple_of(j * 256, 256)
                pre, shifts = conv_pre(raw, conv_w, conv_b, r0, 64, c0, 256)
                dp = d_act[pl.ds(pl.multiple_of(i * 64, 64), 64), pl.ds(c0, 256)] * silu_slope(pre, jax.nn.sigmoid(pre))
                d_pre[pl.ds(r0, 64), pl.ds(c0, 256)] = dp.astype(BF16)
                for k in range(len(shifts)):
                    w_acc[k, :, pl.ds(c0, 256)] += jnp.sum((dp * shifts[k]).reshape(8, 8, 256), axis=0)
                w_acc[len(shifts), :, pl.ds(c0, 256)] += jnp.sum(dp.reshape(8, 8, 256), axis=0)
                return 0

            return lax.fori_loop(0, conv_ch // 256, conv_cols, 0)

        lax.fori_loop(0, CHUNK // 64, conv_tile, 0)
        return 0

    lax.fori_loop(0, chunks, chunk, 0)
    taps = w_grad.shape[0]
    for k in range(taps):
        w_grad[k : k + 1, :] = jnp.sum(w_acc[k], axis=0, keepdims=True)
    b_grad[...] = jnp.sum(w_acc[taps], axis=0, keepdims=True)


def input_kernel(tok, og, normed, w_in, gain, conv_w, dgate, d_pre, d_dt,
                 in_grad, gw_in, gain_grad, d_raw, dn, acc):
    length, inner = dgate.shape
    ext, d = tok.shape
    conv_ch = d_pre.shape[1]
    proj = w_in.shape[1]
    heads = proj - inner - conv_ch
    taps = conv_w.shape[0]

    def conv_tile(i, _):
        r0 = pl.multiple_of(i * 64, 64)

        def conv_cols(j, _):
            c0 = pl.multiple_of(j * 256, 256)
            window = d_pre[pl.ds(r0, 64 + HALO), pl.ds(c0, 256)].astype(F32)
            total = jnp.zeros((64, 256), F32)
            for k in range(taps):
                off = taps - 1 - k
                total = total + conv_w[k : k + 1, pl.ds(c0, 256)] * window[off : off + 64]
            d_raw[pl.ds(r0, 64), pl.ds(c0, 256)] = total.astype(BF16)
            return 0

        return lax.fori_loop(0, conv_ch // 256, conv_cols, 0)

    lax.fori_loop(0, length // 64, conv_tile, 0)
    d_raw[:, conv_ch : conv_ch + LANES] = d_dt[...].astype(BF16)
    acc[...] = jnp.zeros_like(acc)

    def grad_rows(i, _):
        rows = pl.ds(pl.multiple_of(i * CHUNK, CHUNK), CHUNK)
        total = dot(dgate[rows, :], w_in[:, 0:inner], LAST)
        dn[...] = total + dot(d_raw[rows, 0 : conv_ch + heads], w_in[:, inner:], LAST)

        def rows16(j, _):
            sub = pl.ds(pl.multiple_of(j * 16, 16), 16)
            at = pl.ds(pl.multiple_of(i * CHUNK + j * 16, 16), 16)
            t = tok[pl.ds(pl.multiple_of(i * CHUNK + j * 16 + HALO, 16), 16), :].astype(F32)
            r = lax.rsqrt(jnp.mean(t * t, axis=-1, keepdims=True) + EPSILON)
            unit = t * r
            g = dn[sub, :]
            both = g * unit
            acc[...] = acc[...] + both[0:8] + both[8:16]
            scaled = g * gain[...]
            back = r * (scaled - unit * jnp.mean(unit * scaled, axis=-1, keepdims=True))
            in_grad[at, :] = (og[at, :].astype(F32) + back).astype(in_grad.dtype)
            return 0

        return lax.fori_loop(0, CHUNK // 16, rows16, 0)

    lax.fori_loop(0, length // CHUNK, grad_rows, 0)
    gain_grad[...] = jnp.sum(acc[...], axis=0, keepdims=True)

    def w_rows(i, _):
        cols = pl.ds(pl.multiple_of(i * 128, 128), 128)
        n = normed[pl.ds(HALO, length), cols]
        gw_in[cols, 0:inner] = dot(n, dgate[...], ROWS)
        gw_in[cols, inner:] = dot(n, d_raw[:, 0 : conv_ch + heads], ROWS)
        return 0

    lax.fori_loop(0, d // 128, w_rows, 0)


def vmem_call(kernel, outs, scratch, name):
    spec = pl.BlockSpec(memory_space=pltpu.VMEM)

    def run(*args):
        return pl.pallas_call(
            kernel,
            out_shape=[jax.ShapeDtypeStruct(s, t) for s, t in outs],
            in_specs=[spec] * len(args),
            out_specs=[spec] * len(outs),
            scratch_shapes=[pltpu.VMEM(s, t) for s, t in scratch],
            compiler_params=pltpu.CompilerParams(vmem_limit_bytes=VMEM_LIMIT),
            name=name,
        )(*args)

    return run


def shards(block_in, gain_in, w_in, conv_w, conv_b, dt_bias, a_log, d_skip, gain_out, w_out, out_grad):
    both = ("shard", "head")
    ranges, groups = lax.axis_size("shard"), lax.axis_size("head")
    head_index = lax.axis_index("head")
    seqs, segment, d = block_in.shape
    inner = gain_out.shape[0]
    heads = dt_bias.shape[0]
    conv_ch = conv_b.shape[0]
    taps = conv_w.shape[0]
    state_n = (conv_ch - inner) // 2
    parts = groups // seqs
    length = segment * (groups // parts)
    chunks = length // CHUNK
    ext = length + HALO
    members = [(s, h) for s in range(ranges) for h in range(groups)]
    index = {m: i for i, m in enumerate(members)}

    def after(s, h):
        return (s, h + 1) if (h + 1) % parts else (s + 1, h + 1 - parts)

    forth = [(index[m], index[after(*m)]) for m in members if after(*m) in index]
    back = [(b, a) for a, b in forth]

    def to_ranges(array):
        if parts == 1:
            return lax.all_to_all(array, "head", split_axis=0, concat_axis=1, tiled=True)[0]
        everything = lax.all_gather(array, "head", axis=1, tiled=True)
        mine = lax.dynamic_index_in_dim(everything, head_index // parts, 0, False)
        return lax.dynamic_slice_in_dim(mine, (head_index % parts) * length, length, 0)

    def to_blocks(array):
        if parts == 1:
            return lax.all_to_all(array[None], "head", split_axis=1, concat_axis=0, tiled=True)
        everything = lax.all_gather(array, "head", axis=0, tiled=True).reshape(seqs, groups * segment, -1)
        return lax.dynamic_slice_in_dim(everything, head_index * segment, segment, 1)

    def chain(own, decay, route):
        def hop(_, before):
            return lax.ppermute((decay * before.astype(F32) + own).astype(BF16), both, route)

        return lax.fori_loop(0, ranges * parts - 1, hop, jnp.zeros(own.shape, BF16)).astype(F32)

    full_in = lax.all_gather(w_in, both, axis=0, tiled=True)
    full_out = lax.all_gather(w_out, both, axis=0, tiled=True)
    tok = to_ranges(block_in)
    og = to_ranges(out_grad)
    tok = jnp.concatenate([lax.ppermute(tok[-HALO:], both, forth), tok], axis=0)

    pad = LANES - heads
    gain_in_row, gain_out_row, conv_b_row = gain_in[None], gain_out[None], conv_b[None]
    bias_row = jnp.pad(dt_bias, (0, pad))[None]
    rate_row = jnp.pad(a_log, (0, pad), constant_values=-1e30)[None]
    skip_row = jnp.repeat(d_skip, inner // heads)[None]

    normed, gate, raw, dt_raw, act, dt, cum, cum_t, loc, dec = vmem_call(
        project_kernel,
        [
            ((ext, d), BF16), ((ext, inner), BF16), ((ext, conv_ch), BF16), ((ext, LANES), F32), ((length, conv_ch), BF16),
            ((length, LANES), F32), ((length, LANES), F32), ((chunks, LANES, CHUNK), F32),
            ((chunks + 1, state_n, inner), F32), ((1, LANES), F32),
        ],
        [((2 * LANES, inner), BF16), ((state_n, inner), F32)],
        "project",
    )(tok, full_in, gain_in_row, conv_w, conv_b_row, bias_row, rate_row)

    decay = jnp.repeat(jnp.exp(dec[0, :heads]), inner // heads)[None]
    enter = chain(loc[chunks], decay, forth)

    out, dy, dgate, gw_out, g_gain_out, g_skip, y_dot, states, direct, leave = vmem_call(
        mix_kernel,
        [
            ((length, d), BF16), ((length, inner), BF16), ((length, inner), BF16), ((inner, d), F32), ((1, inner), F32),
            ((1, LANES), F32), ((length, LANES), F32), ((chunks + 1, state_n, inner), F32),
            ((chunks, state_n, inner), F32), ((state_n, inner), F32),
        ],
        [
            ((2 * LANES, inner), BF16), ((CHUNK, inner), F32), ((CHUNK, inner), BF16), ((length, inner), BF16),
            ((CHUNK, inner), F32), ((8, inner), F32),
        ],
        "mix",
    )(tok, og, full_out, gate, act, dt, cum, cum_t, loc, enter, gain_out_row, skip_row)

    leaving = chain(leave, decay, back)

    d_pre, d_dt, g_conv_w, g_conv_b, g_bias, g_rate = vmem_call(
        back_kernel,
        [
            ((ext, conv_ch), BF16), ((length, LANES), F32), ((taps, conv_ch), F32), ((1, conv_ch), F32),
            ((1, LANES), F32), ((1, LANES), F32),
        ],
        [
            ((2 * LANES, inner), BF16), ((CHUNK, inner), BF16), ((CHUNK, inner), F32), ((CHUNK, conv_ch), F32),
            ((state_n, inner), F32), ((taps + 1, 8, conv_ch), F32),
        ],
        "back",
    )(raw, dt_raw, act, dt, cum, cum_t, dy, states, direct, leaving, y_dot, conv_w, conv_b_row, bias_row, rate_row, skip_row)

    d_pre = d_pre.at[length:].set(lax.ppermute(d_pre[:HALO], both, back))

    in_grad, gw_in, g_gain_in = vmem_call(
        input_kernel,
        [((length, d), BF16), ((d, w_in.shape[1]), F32), ((1, d), F32)],
        [((length, conv_ch + LANES), BF16), ((CHUNK, d), F32), ((8, d), F32)],
        "input",
    )(tok, og, normed, full_in, gain_in_row, conv_w, dgate, d_pre, d_dt)

    owned_in = lax.psum_scatter(gw_in, both, scatter_dimension=0, tiled=True)
    owned_out = lax.psum_scatter(gw_out, both, scatter_dimension=0, tiled=True)
    small = lax.psum(
        (g_gain_in[0], g_gain_out[0], g_conv_w, g_conv_b[0], g_bias[0, :heads], g_rate[0, :heads], g_skip[0, :heads]), both
    )
    return (
        to_blocks(out),
        to_blocks(in_grad).astype(F32),
        small[0],
        owned_in,
        small[2],
        small[3],
        small[4],
        small[5],
        small[6],
        small[1],
        owned_out,
    )


def solution(mesh):
    rows, tokens = P(("shard", "head"), None), P(None, ("shard", "head"), None)
    return jax.shard_map(
        shards,
        mesh=mesh,
        in_specs=(tokens, P(), rows, P(), P(), P(), P(), P(), P(), rows, tokens),
        out_specs=(tokens, tokens, P(), rows, P(), P(), P(), P(), P(), P(), rows),
        check_vma=False,
    )
```

time: 1460 us -> 509 us (0.35); the launches traced: 1440 us -> 508 us
  local copies, waits for them, and re-layouts: 453 us -> 19.1 us
  other arithmetic: 308 us -> 15.2 us
  matrix products: 185 us -> 0 us
  Pallas kernels: 0 us -> 108 us
  blocking collectives: 143 us -> 52.1 us
  waiting for transfers between devices: 306 us -> 222 us
  starting transfers between devices: 25.2 us -> 76.9 us
    dynamic_update_slice x161 -> x0, local copies, waits for them, and re-layouts: 254 us -> none  [the longest x36 148 us: shards(): lax.map(local_backward, (padded_x, padded_bc, dt_in, entering, mixed_back...]
    dot_general x104 -> x0, matrix products: 185 us -> none  [the longest x18 56.1 us: advance(): inside = jnp.einsum('tsh,shp->thp', mixing, x_block, precision=HIGHEST)]
    pallas_call x0 -> x4, Pallas kernels: none -> 108 us  [run(): pl.pallas_call(kernel, out_shape=[jax.ShapeDtypeStruct(s, t) for s, t in...]
    all_gather x5 -> x2, waiting for transfers between devices: 150 us -> 44.8 us  [the longest x1 44.8 us: shards(): full_in = lax.all_gather(w_in, both, axis=0, tiled=True)]
    another operation x111 -> x0, other arithmetic: 101 us -> none
    all_to_all x2 -> x0, blocking collectives: 89.7 us -> none  [the longest x1 48.9 us: shards(): lax.all_to_all(mixed, 'head', split_axis=1, concat_axis=2, tiled=True)]
    ppermute x4 -> x16, waiting for transfers between devices: 0.63 us -> 78.9 us  [the longest x14 71.6 us: hop(): lax.ppermute((decay * before.astype(F32) + own).astype(BF16), both, route)]
    reduce_sum x54 -> x0, other arithmetic: 72 us -> none  [the longest x8 17.9 us: causal_conv(): taps_weight[offset][None, :] * padded[offset:offset + length]]
  transfers between devices with their start and end apart: 16 -> 24, of which waited for: 11 -> 19; matrix products, arithmetic and copies ran while one was open for 57% -> 6% of each run, Pallas kernels for 0% -> 15%
where the time goes in v1:
time: 509 us; the launch traced here: 508 us
  waiting for transfers between devices  222 us (44%)
  Pallas kernels  108 us (21%)
  starting transfers between devices  76.9 us (15%)
  blocking collectives  52.1 us (10%)
  local copies, waits for them, and re-layouts  19.1 us (4%)
  other arithmetic  15.2 us (3%)
  between operations  14.1 us (3%)
    pallas_call x4, Pallas kernels, run(): pl.pallas_call(kernel, out_shape=[jax.ShapeDtypeStruct(s, t) for s, t in...  108 us
    ppermute x14, waiting for transfers between devices, hop(): lax.ppermute((decay * before.astype(F32) + own).astype(BF16), both, route)  71.6 us
    unnamed x5, waiting for transfers between devices  63.2 us
    ppermute x14, starting transfers between devices, hop(): lax.ppermute((decay * before.astype(F32) + own).astype(BF16), both, route)  56.9 us
    psum x1, blocking collectives, shards(): lax.psum((g_gain_in[0], g_gain_out[0], g_conv_w, g_conv_b[0], g_bias[0, :...  52.1 us
    all_gather x1, waiting for transfers between devices, shards(): full_in = lax.all_gather(w_in, both, axis=0, tiled=True)  44.8 us
    all_to_all x2, waiting for transfers between devices, to_ranges(): lax.all_to_all(array, 'head', split_axis=0, concat_axis=1, tiled=True)[0]  22.9 us
    all_to_all x2, waiting for transfers between devices, to_blocks(): lax.all_to_all(array[None], 'head', split_axis=1, concat_axis=0, tiled=True)  12.5 us
  transfers between devices with their start and end apart: 24, of which 19 were waited for; matrix products, arithmetic and copies ran while one was open for 6% of the time, Pallas kernels for 15%

profile of v1, /device:TPU:0, one launch (start us, length us, event | category | flops | bytes accessed | tf_op | source)
XLA Modules:
  0.0 507.6 jit_solution(172745520718096021)
XLA Ops:
  8.0 6.4 %all-to-all-start = ((bf16[4,128,768]{2,1,0:T(8,128)(2,1)}), bf16[4,128,768]{2,1,0:T(8,128)(2,1)S(1)}, u32[]{:S(2)}, u32[]{:S(2)}) async-start(bf16[4,128,768]{2,1,0:T(8,128)(2,1)} %param.17), calls=%async_computation | async-start | bytes 1572864 | tf_op jit(solution)/shard_map/all_to_all | solution.py:458
  14.3 0.7 all-gather.3.cloned.1.call-update
  15.1 22.9 %all-to-all-done = bf16[4,128,768]{2,1,0:T(8,128)(2,1)S(1)} async-done(((bf16[4,128,768]{2,1,0:T(8,128)(2,1)}), bf16[4,128,768]{2,1,0:T(8,128)(2,1)S(1)}, u32[]{:S(2)}, u32[]{:S(2)}) %all-to-all-start) | async-done | bytes 786464 | tf_op jit(solution)/shard_map/all_to_all | solution.py:458
  37.9 3.5 all-to-all-start.1
  41.5 1.3 collective-permute-start.2
  45.9 0.9 pad_maximum_fusion.tok
  46.8 44.8 %all-gather.5.cloned.1.call-done.w_in = bf16[768,3352]{1,0:T(8,128)(2,1)} async-done(((bf16[24,3352]{1,0:T(8,128)(2,1)}), bf16[768,3352]{1,0:T(8,128)(2,1)}) %all-gather.5.cloned.1.call-update) | async-done | bytes 5148688 | tf_op jit(solution)/shard_map/all_gather | solution.py:475
  91.6 23.0 %project.1 = (bf16[528,768]{1,0:T(8,128)(2,1)}, bf16[528,1536]{1,0:T(8,128)(2,1)}, bf16[528,1792]{1,0:T(8,128)(2,1)}, f32[528,128]{1,0:T(8,128)}, bf16[512,1792]...) custom-call(bf16[528,768]{1,0:T(8,128)(2,1)} %pad_maximum_fusion.tok, ...), custom_call_target="tpu_custom_call" | custom-call | tf_op jit(solution)/shard_map/project/pallas_call | solution.py:420
  115.3 1.2 slice_bitcast_fusion
  116.5 58.8 %while.23 = (s32[]{:T(128)}, bf16[128,1536]{1,0:T(8,128)(2,1)S(1)}, f32[128,1536]{1,0:T(8,128)S(1)}, f32[24]{0:T(128)S(1)}, s32[]{:T(128)}) while((s32[]{:T(128)}, bf16[128,1536]{1,0:T(8,128)(2,1)S(1)}, f32[128,1536]{1,0:T(8,128)S(1)}, f32[24]{0:T(128)S(1)}, s32[]{:T(128)}) %tuple.46), condition=%wide.region_1.2_spmd.clone, body=%wide.region_0.1_spmd.clone.sunk | while | flops 786434 | bytes 3170501 | solution.py:473
  116.8 2.2 collective-permute-start
  119.0 1.3 collective-permute-done
  120.5 6.6 %collective-permute-start = (bf16[128,1536]{1,0:T(8,128)(2,1)S(1)}, bf16[128,1536]{1,0:T(8,128)(2,1)S(1)}, u32[]{:S(2)}, u32[]{:S(2)}) collective-permute-start(bf16[128,1536]{1,0:T(8,128)(2,1)S(1)} %add_convert_fusion.4), channel_id=1, source_target_pairs={{0,4},{1,5},{2,6},{3,7},{4,8},{5,9},{6,10},{7,11},{8,12},{9,13},{1... | collective-permute-start | bytes 1179656 | tf_op jit(solution)/shard_map/while/body/eval_jaxpr/ppermute | solution.py:471
  127.2 1.3 collective-permute-done
  128.7 7.8 %collective-permute-start = (bf16[128,1536]{1,0:T(8,128)(2,1)S(1)}, bf16[128,1536]{1,0:T(8,128)(2,1)S(1)}, u32[]{:S(2)}, u32[]{:S(2)}) collective-permute-start(bf16[128,1536]{1,0:T(8,128)(2,1)S(1)} %add_convert_fusion.4), channel_id=1, source_target_pairs={{0,4},{1,5},{2,6},{3,7},{4,8},{5,9},{6,10},{7,11},{8,12},{9,13},{1... | collective-permute-start | bytes 1179656 | tf_op jit(solution)/shard_map/while/body/eval_jaxpr/ppermute | solution.py:471
  136.5 1.3 collective-permute-done
  138.0 8.0 %collective-permute-start = (bf16[128,1536]{1,0:T(8,128)(2,1)S(1)}, bf16[128,1536]{1,0:T(8,128)(2,1)S(1)}, u32[]{:S(2)}, u32[]{:S(2)}) collective-permute-start(bf16[128,1536]{1,0:T(8,128)(2,1)S(1)} %add_convert_fusion.4), channel_id=1, source_target_pairs={{0,4},{1,5},{2,6},{3,7},{4,8},{5,9},{6,10},{7,11},{8,12},{9,13},{1... | collective-permute-start | bytes 1179656 | tf_op jit(solution)/shard_map/while/body/eval_jaxpr/ppermute | solution.py:471
  146.0 1.3 collective-permute-done
  147.6 7.7 %collective-permute-start = (bf16[128,1536]{1,0:T(8,128)(2,1)S(1)}, bf16[128,1536]{1,0:T(8,128)(2,1)S(1)}, u32[]{:S(2)}, u32[]{:S(2)}) collective-permute-start(bf16[128,1536]{1,0:T(8,128)(2,1)S(1)} %add_convert_fusion.4), channel_id=1, source_target_pairs={{0,4},{1,5},{2,6},{3,7},{4,8},{5,9},{6,10},{7,11},{8,12},{9,13},{1... | collective-permute-start | bytes 1179656 | tf_op jit(solution)/shard_map/while/body/eval_jaxpr/ppermute | solution.py:471
  155.4 1.3 collective-permute-done
  156.9 7.8 %collective-permute-start = (bf16[128,1536]{1,0:T(8,128)(2,1)S(1)}, bf16[128,1536]{1,0:T(8,128)(2,1)S(1)}, u32[]{:S(2)}, u32[]{:S(2)}) collective-permute-start(bf16[128,1536]{1,0:T(8,128)(2,1)S(1)} %add_convert_fusion.4), channel_id=1, source_target_pairs={{0,4},{1,5},{2,6},{3,7},{4,8},{5,9},{6,10},{7,11},{8,12},{9,13},{1... | collective-permute-start | bytes 1179656 | tf_op jit(solution)/shard_map/while/body/eval_jaxpr/ppermute | solution.py:471
  164.7 1.3 collective-permute-done
  166.3 7.8 %collective-permute-start = (bf16[128,1536]{1,0:T(8,128)(2,1)S(1)}, bf16[128,1536]{1,0:T(8,128)(2,1)S(1)}, u32[]{:S(2)}, u32[]{:S(2)}) collective-permute-start(bf16[128,1536]{1,0:T(8,128)(2,1)S(1)} %add_convert_fusion.4), channel_id=1, source_target_pairs={{0,4},{1,5},{2,6},{3,7},{4,8},{5,9},{6,10},{7,11},{8,12},{9,13},{1... | collective-permute-start | bytes 1179656 | tf_op jit(solution)/shard_map/while/body/eval_jaxpr/ppermute | solution.py:471
  174.1 1.3 collective-permute-done
  175.4 1.0 convert_element_type.26.enter
  176.3 0.9 copy-done
  177.2 33.7 %mix.1 = (bf16[512,768]{1,0:T(8,128)(2,1)}, bf16[512,1536]{1,0:T(8,128)(2,1)}, bf16[512,1536]{1,0:T(8,128)(2,1)}, f32[1536,768]{1,0:T(8,128)}, f32[1,1536]{1,0:T...) custom-call(bf16[528,768]{1,0:T(8,128)(2,1)} %pad_maximum_fusion.tok, ...), custom_call_target="tpu_custom_call" | custom-call | tf_op jit(solution)/shard_map/mix/pallas_call | solution.py:420
  211.1 73.4 %while.24 = (s32[]{:T(128)}, bf16[128,1536]{1,0:T(8,128)(2,1)S(1)}, f32[128,1536]{1,0:T(8,128)S(1)}, f32[24]{0:T(128)S(1)}, s32[]{:T(128)}) while((s32[]{:T(128)}, bf16[128,1536]{1,0:T(8,128)(2,1)S(1)}, f32[128,1536]{1,0:T(8,128)S(1)}, f32[24]{0:T(128)S(1)}, s32[]{:T(128)}) %tuple.60), condition=%wide.region_3.4_spmd.clone, body=%wide.region_2.3_spmd.clone.sunk | while | flops 786434 | bytes 3170501 | solution.py:473
  211.3 1.3 collective-permute-start.1
  212.6 7.7 %collective-permute-done.1 = bf16[128,1536]{1,0:T(8,128)(2,1)S(1)} collective-permute-done((bf16[128,1536]{1,0:T(8,128)(2,1)S(1)}, bf16[128,1536]{1,0:T(8,128)(2,1)S(1)}, u32[]{:S(2)}, u32[]{:S(2)}) %collective-permute-start.1) | collective-permute-done | bytes 393248 | tf_op jit(solution)/shard_map/while/body/eval_jaxpr/ppermute | solution.py:471
  220.5 1.3 collective-permute-start.1
  221.8 8.5 %collective-permute-done.1 = bf16[128,1536]{1,0:T(8,128)(2,1)S(1)} collective-permute-done((bf16[128,1536]{1,0:T(8,128)(2,1)S(1)}, bf16[128,1536]{1,0:T(8,128)(2,1)S(1)}, u32[]{:S(2)}, u32[]{:S(2)}) %collective-permute-start.1) | collective-permute-done | bytes 393248 | tf_op jit(solution)/shard_map/while/body/eval_jaxpr/ppermute | solution.py:471
  230.6 1.3 collective-permute-start.1
  231.9 7.8 %collective-permute-done.1 = bf16[128,1536]{1,0:T(8,128)(2,1)S(1)} collective-permute-done((bf16[128,1536]{1,0:T(8,128)(2,1)S(1)}, bf16[128,1536]{1,0:T(8,128)(2,1)S(1)}, u32[]{:S(2)}, u32[]{:S(2)}) %collective-permute-start.1) | collective-permute-done | bytes 393248 | tf_op jit(solution)/shard_map/while/body/eval_jaxpr/ppermute | solution.py:471
  240.0 1.3 collective-permute-start.1
  241.3 7.9 %collective-permute-done.1 = bf16[128,1536]{1,0:T(8,128)(2,1)S(1)} collective-permute-done((bf16[128,1536]{1,0:T(8,128)(2,1)S(1)}, bf16[128,1536]{1,0:T(8,128)(2,1)S(1)}, u32[]{:S(2)}, u32[]{:S(2)}) %collective-permute-start.1) | collective-permute-done | bytes 393248 | tf_op jit(solution)/shard_map/while/body/eval_jaxpr/ppermute | solution.py:471
  249.5 1.3 collective-permute-start.1
  250.8 8.8 %collective-permute-done.1 = bf16[128,1536]{1,0:T(8,128)(2,1)S(1)} collective-permute-done((bf16[128,1536]{1,0:T(8,128)(2,1)S(1)}, bf16[128,1536]{1,0:T(8,128)(2,1)S(1)}, u32[]{:S(2)}, u32[]{:S(2)}) %collective-permute-start.1) | collective-permute-done | bytes 393248 | tf_op jit(solution)/shard_map/while/body/eval_jaxpr/ppermute | solution.py:471
  259.9 1.3 collective-permute-start.1
  261.2 8.6 %collective-permute-done.1 = bf16[128,1536]{1,0:T(8,128)(2,1)S(1)} collective-permute-done((bf16[128,1536]{1,0:T(8,128)(2,1)S(1)}, bf16[128,1536]{1,0:T(8,128)(2,1)S(1)}, u32[]{:S(2)}, u32[]{:S(2)}) %collective-permute-start.1) | collective-permute-done | bytes 393248 | tf_op jit(solution)/shard_map/while/body/eval_jaxpr/ppermute | solution.py:471
  270.0 1.3 collective-permute-start.1
  271.3 13.1 %collective-permute-done.1 = bf16[128,1536]{1,0:T(8,128)(2,1)S(1)} collective-permute-done((bf16[128,1536]{1,0:T(8,128)(2,1)S(1)}, bf16[128,1536]{1,0:T(8,128)(2,1)S(1)}, u32[]{:S(2)}, u32[]{:S(2)}) %collective-permute-start.1) | collective-permute-done | bytes 393248 | tf_op jit(solution)/shard_map/while/body/eval_jaxpr/ppermute | solution.py:471
  284.4 1.0 convert_element_type.27.leaving
  285.4 22.8 %back.1 = (bf16[528,1792]{1,0:T(8,128)(2,1)}, f32[512,128]{1,0:T(8,128)}, f32[4,1792]{1,0:T(4,128)}, f32[1,1792]{1,0:T(1,128)}, f32[1,128]{1,0:T(1,128)}, /*index=5*/f32[1,128]{1,0:T(1,128)}) custom-call(bf16[528,1792]{1,0:T(8,128)(2,1)} %get-tuple-element.107.raw, f32[528,128]{1,0:T(8,128)} %get-tuple-element.108.dt_raw, ...), custom_call_target="tpu_custom_call" | custom-call | tf_op jit(solution)/shard_map/back/pallas_call | solution.py:420
  308.2 0.8 slice.41
  309.0 1.5 collective-permute-start.3
  310.5 7.3 %collective-permute-done.3 = bf16[16,1792]{1,0:T(8,128)(2,1)S(1)} collective-permute-done((bf16[16,1792]{1,0:T(8,128)(2,1)S(1)}, bf16[16,1792]{1,0:T(8,128)(2,1)S(1)}, u32[]{:S(2)}, u32[]{:S(2)}) %collective-permute-start.3) | collective-permute-done | bytes 57376 | tf_op jit(solution)/shard_map/ppermute | solution.py:530
  318.4 28.0 %input.1 = (bf16[512,768]{1,0:T(8,128)(2,1)}, f32[768,3352]{1,0:T(8,128)}, f32[1,768]{1,0:T(1,128)}) custom-call(bf16[528,768]{1,0:T(8,128)(2,1)} %pad_maximum_fusion.tok, bf16[512,768]{1,0:T(8,128)(2,1)} %bitcast.29, bf16[528,768]{1,0:T(8,128)(2,1)} %get-tuple-element.105.normed, bf16[768,3352]{1,0:T(8,128)(2,1)} %all-gather.5.cloned.1.call-done.w_in, ...), custom_call_target="tpu_custom_call" | custom-call | tf_op jit(solution)/shard_map/input/pallas_call | solution.py:420
  346.5 1.1 copy-done.1
  347.6 1.2 copy.31
  349.3 5.4 %reduce.5 = bf16[512,768]{1,0:T(8,128)(2,1)S(1)} reduce(bf16[512,1,768]{2,1,0:T(2,128)(2,1)S(1)} %bitcast.30, bf16[]{:T(256)} %broadcast.26), dimensions={1}, to_apply=%bitcast.27.reduce_sub_computation | reduce | bytes 1572866
  354.7 1.0 reshape.71
  355.7 3.7 all-to-all-start.2
  359.5 1.2 copy.30
  360.7 5.4 %reduce.6 = bf16[512,768]{1,0:T(8,128)(2,1)S(1)} reduce(bf16[512,1,768]{2,1,0:T(2,128)(2,1)S(1)} %bitcast.31, bf16[]{:T(256)} %broadcast.26), dimensions={1}, to_apply=%bitcast.26.reduce_sub_computation | reduce | bytes 1572866
  366.2 1.0 reshape.73
  367.2 12.5 %all-to-all-done.2 = bf16[4,2,49152]{2,1,0:T(2,128)(2,1)S(1)} async-done(((bf16[4,2,49152]{2,1,0:T(2,128)(2,1)}), bf16[4,2,49152]{2,1,0:T(2,128)(2,1)S(1)}, u32[]{:S(2)}, u32[]{:S(2)}) %all-to-all-start.2) | async-done | bytes 786464 | tf_op jit(solution)/shard_map/all_to_all | solution.py:465
  379.7 3.5 all-to-all-start.3
  383.4 52.1 %all-reduce.3 = (f32[768]{0:T(1024)}, f32[4,1792]{1,0:T(4,128)}, f32[1792]{0:T(1024)}, f32[24]{0:T(128)}, f32[24]{0:T(128)}, /*index=5*/f32[24]{0:T(128)}, f32[1536]{0:T(1024)}) all-reduce(f32[768]{0:T(1024)S(1)} %reduce.2, f32[4,1792]{1,0:T(4,128)S(1)} %copy-done.3, ...), channel_id=1, replica_groups=mesh['shard'=8,'head'=4] {'shard','head'}, use_global_device_ids=true, to_apply=%region_4.5 | all-reduce | flops 11336 | bytes 90688 | tf_op jit(solution)/shard_map/psum | solution.py:541
  435.6 0.7 reshape.72
  436.3 1.0 copy.26
  437.3 0.7 reshape.74
  438.0 1.2 copy.27
  439.3 61.7 %reduce-scatter.7.cloned.1.call-done = f32[24,3352]{1,0:T(8,128)} async-done(((f32[768,3352]{1,0:T(8,128)}), f32[24,3352]{1,0:T(8,128)}) %reduce-scatter.7.cloned.1.call-update) | async-done | bytes 321808
  (102 shorter events, 9.3 us)
Async XLA Ops:
  7.2 35.6 %copy-start.12 = (f32[24]{0:T(128)S(1)}, f32[24]{0:T(128)}, u32[]{:S(2)}) copy-start(f32[24]{0:T(128)} %param.22) | copy-start | bytes 292
  7.2 35.6 %copy-start.11 = (f32[24]{0:T(128)S(1)}, f32[24]{0:T(128)}, u32[]{:S(2)}) copy-start(f32[24]{0:T(128)} %param.23) | copy-start | bytes 292
  7.2 36.1 %copy-start.5 = (f32[1792]{0:T(1024)S(1)}, f32[1792]{0:T(1024)}, u32[]{:S(2)}) copy-start(f32[1792]{0:T(1024)} %param.21) | copy-start | bytes 21508
  7.2 36.7 %copy-start.8 = (f32[768]{0:T(1024)S(1)}, f32[768]{0:T(1024)}, u32[]{:S(2)}) copy-start(f32[768]{0:T(1024)} %param.18) | copy-start | bytes 9220
  7.2 37.3 %copy-start.10 = (f32[24]{0:T(128)S(1)}, f32[24]{0:T(128)}, u32[]{:S(2)}) copy-start(f32[24]{0:T(128)} %param.24) | copy-start | bytes 292
  7.2 38.0 %copy-start.4 = (f32[1536]{0:T(1024)S(1)}, f32[1536]{0:T(1024)}, u32[]{:S(2)}) copy-start(f32[1536]{0:T(1024)} %param.25) | copy-start | bytes 18436
  7.2 84.4 %all-gather.5.cloned.1.call-start = ((), (), s32[]{:S(2)}) async-start(), calls=%async_computation.7 | async-start | bytes 5474304 | tf_op jit(solution)/shard_map/all_gather | solution.py:475
  8.0 29.9 %all-to-all-start = ((bf16[4,128,768]{2,1,0:T(8,128)(2,1)}), bf16[4,128,768]{2,1,0:T(8,128)(2,1)S(1)}, u32[]{:S(2)}, u32[]{:S(2)}) async-start(bf16[4,128,768]{2,1,0:T(8,128)(2,1)} %param.17), calls=%async_computation | async-start | bytes 1572864 | tf_op jit(solution)/shard_map/all_to_all | solution.py:458
  14.3 162.0 %all-gather.3.cloned.1.call-start = ((), (), s32[]{:S(2)}) async-start(), calls=%async_computation.6 | async-start | bytes 2433024 | tf_op jit(solution)/shard_map/all_gather | solution.py:476
  37.9 138.4 %all-to-all-start.1 = ((bf16[4,128,768]{2,1,0:T(8,128)(2,1)}), bf16[4,128,768]{2,1,0:T(8,128)(2,1)S(1)}, u32[]{:S(2)}, u32[]{:S(2)}) async-start(bf16[4,128,768]{2,1,0:T(8,128)(2,1)} %param.27), calls=%async_computation.1 | async-start | bytes 1572864 | tf_op jit(solution)/shard_map/all_to_all | solution.py:458
  41.4 397.9 %reduce-scatter.5.cloned.1.call-start = ((), (), s32[]{:S(2)}) async-start(), calls=%async_computation.8 | async-start | bytes 4866048 | tf_op jit(solution)/shard_map/reduce_scatter | solution.py:540
  41.5 4.4 collective-permute-start.2
  116.8 3.5 collective-permute-start
  120.5 7.9 %collective-permute-start = (bf16[128,1536]{1,0:T(8,128)(2,1)S(1)}, bf16[128,1536]{1,0:T(8,128)(2,1)S(1)}, u32[]{:S(2)}, u32[]{:S(2)}) collective-permute-start(bf16[128,1536]{1,0:T(8,128)(2,1)S(1)} %add_convert_fusion.4), channel_id=1, source_target_pairs={{0,4},{1,5},{2,6},{3,7},{4,8},{5,9},{6,10},{7,11},{8,12},{9,13},{1... | collective-permute-start | bytes 1179656 | tf_op jit(solution)/shard_map/while/body/eval_jaxpr/ppermute | solution.py:471
  128.7 9.1 %collective-permute-start = (bf16[128,1536]{1,0:T(8,128)(2,1)S(1)}, bf16[128,1536]{1,0:T(8,128)(2,1)S(1)}, u32[]{:S(2)}, u32[]{:S(2)}) collective-permute-start(bf16[128,1536]{1,0:T(8,128)(2,1)S(1)} %add_convert_fusion.4), channel_id=1, source_target_pairs={{0,4},{1,5},{2,6},{3,7},{4,8},{5,9},{6,10},{7,11},{8,12},{9,13},{1... | collective-permute-start | bytes 1179656 | tf_op jit(solution)/shard_map/while/body/eval_jaxpr/ppermute | solution.py:471
  138.0 9.3 %collective-permute-start = (bf16[128,1536]{1,0:T(8,128)(2,1)S(1)}, bf16[128,1536]{1,0:T(8,128)(2,1)S(1)}, u32[]{:S(2)}, u32[]{:S(2)}) collective-permute-start(bf16[128,1536]{1,0:T(8,128)(2,1)S(1)} %add_convert_fusion.4), channel_id=1, source_target_pairs={{0,4},{1,5},{2,6},{3,7},{4,8},{5,9},{6,10},{7,11},{8,12},{9,13},{1... | collective-permute-start | bytes 1179656 | tf_op jit(solution)/shard_map/while/body/eval_jaxpr/ppermute | solution.py:471
  147.6 9.1 %collective-permute-start = (bf16[128,1536]{1,0:T(8,128)(2,1)S(1)}, bf16[128,1536]{1,0:T(8,128)(2,1)S(1)}, u32[]{:S(2)}, u32[]{:S(2)}) collective-permute-start(bf16[128,1536]{1,0:T(8,128)(2,1)S(1)} %add_convert_fusion.4), channel_id=1, source_target_pairs={{0,4},{1,5},{2,6},{3,7},{4,8},{5,9},{6,10},{7,11},{8,12},{9,13},{1... | collective-permute-start | bytes 1179656 | tf_op jit(solution)/shard_map/while/body/eval_jaxpr/ppermute | solution.py:471
  156.9 9.1 %collective-permute-start = (bf16[128,1536]{1,0:T(8,128)(2,1)S(1)}, bf16[128,1536]{1,0:T(8,128)(2,1)S(1)}, u32[]{:S(2)}, u32[]{:S(2)}) collective-permute-start(bf16[128,1536]{1,0:T(8,128)(2,1)S(1)} %add_convert_fusion.4), channel_id=1, source_target_pairs={{0,4},{1,5},{2,6},{3,7},{4,8},{5,9},{6,10},{7,11},{8,12},{9,13},{1... | collective-permute-start | bytes 1179656 | tf_op jit(solution)/shard_map/while/body/eval_jaxpr/ppermute | solution.py:471
  166.3 9.1 %collective-permute-start = (bf16[128,1536]{1,0:T(8,128)(2,1)S(1)}, bf16[128,1536]{1,0:T(8,128)(2,1)S(1)}, u32[]{:S(2)}, u32[]{:S(2)}) collective-permute-start(bf16[128,1536]{1,0:T(8,128)(2,1)S(1)} %add_convert_fusion.4), channel_id=1, source_target_pairs={{0,4},{1,5},{2,6},{3,7},{4,8},{5,9},{6,10},{7,11},{8,12},{9,13},{1... | collective-permute-start | bytes 1179656 | tf_op jit(solution)/shard_map/while/body/eval_jaxpr/ppermute | solution.py:471
  176.3 0.9 copy-start
  211.0 290.1 %reduce-scatter.7.cloned.1.call-start = ((), (), s32[]{:S(2)}) async-start(), calls=%async_computation.9 | async-start | bytes 10948608
  211.3 9.0 %collective-permute-start.1 = (bf16[128,1536]{1,0:T(8,128)(2,1)S(1)}, bf16[128,1536]{1,0:T(8,128)(2,1)S(1)}, u32[]{:S(2)}, u32[]{:S(2)}) collective-permute-start(bf16[128,1536]{1,0:T(8,128)(2,1)S(1)} %add_convert_fusion.5), channel_id=1, source_target_pairs={{4,0},{5,1},{6,2},{7,3},{8,4},{9,5},{10,6},{11,7},{12,8},{13,9},{1... | collective-permute-start | bytes 1179656 | tf_op jit(solution)/shard_map/while/body/eval_jaxpr/ppermute | solution.py:471
  220.5 9.8 %collective-permute-start.1 = (bf16[128,1536]{1,0:T(8,128)(2,1)S(1)}, bf16[128,1536]{1,0:T(8,128)(2,1)S(1)}, u32[]{:S(2)}, u32[]{:S(2)}) collective-permute-start(bf16[128,1536]{1,0:T(8,128)(2,1)S(1)} %add_convert_fusion.5), channel_id=1, source_target_pairs={{4,0},{5,1},{6,2},{7,3},{8,4},{9,5},{10,6},{11,7},{12,8},{13,9},{1... | collective-permute-start | bytes 1179656 | tf_op jit(solution)/shard_map/while/body/eval_jaxpr/ppermute | solution.py:471
  230.6 9.1 %collective-permute-start.1 = (bf16[128,1536]{1,0:T(8,128)(2,1)S(1)}, bf16[128,1536]{1,0:T(8,128)(2,1)S(1)}, u32[]{:S(2)}, u32[]{:S(2)}) collective-permute-start(bf16[128,1536]{1,0:T(8,128)(2,1)S(1)} %add_convert_fusion.5), channel_id=1, source_target_pairs={{4,0},{5,1},{6,2},{7,3},{8,4},{9,5},{10,6},{11,7},{12,8},{13,9},{1... | collective-permute-start | bytes 1179656 | tf_op jit(solution)/shard_map/while/body/eval_jaxpr/ppermute | solution.py:471
  240.0 9.3 %collective-permute-start.1 = (bf16[128,1536]{1,0:T(8,128)(2,1)S(1)}, bf16[128,1536]{1,0:T(8,128)(2,1)S(1)}, u32[]{:S(2)}, u32[]{:S(2)}) collective-permute-start(bf16[128,1536]{1,0:T(8,128)(2,1)S(1)} %add_convert_fusion.5), channel_id=1, source_target_pairs={{4,0},{5,1},{6,2},{7,3},{8,4},{9,5},{10,6},{11,7},{12,8},{13,9},{1... | collective-permute-start | bytes 1179656 | tf_op jit(solution)/shard_map/while/body/eval_jaxpr/ppermute | solution.py:471
  249.5 10.1 %collective-permute-start.1 = (bf16[128,1536]{1,0:T(8,128)(2,1)S(1)}, bf16[128,1536]{1,0:T(8,128)(2,1)S(1)}, u32[]{:S(2)}, u32[]{:S(2)}) collective-permute-start(bf16[128,1536]{1,0:T(8,128)(2,1)S(1)} %add_convert_fusion.5), channel_id=1, source_target_pairs={{4,0},{5,1},{6,2},{7,3},{8,4},{9,5},{10,6},{11,7},{12,8},{13,9},{1... | collective-permute-start | bytes 1179656 | tf_op jit(solution)/shard_map/while/body/eval_jaxpr/ppermute | solution.py:471
  259.9 9.9 %collective-permute-start.1 = (bf16[128,1536]{1,0:T(8,128)(2,1)S(1)}, bf16[128,1536]{1,0:T(8,128)(2,1)S(1)}, u32[]{:S(2)}, u32[]{:S(2)}) collective-permute-start(bf16[128,1536]{1,0:T(8,128)(2,1)S(1)} %add_convert_fusion.5), channel_id=1, source_target_pairs={{4,0},{5,1},{6,2},{7,3},{8,4},{9,5},{10,6},{11,7},{12,8},{13,9},{1... | collective-permute-start | bytes 1179656 | tf_op jit(solution)/shard_map/while/body/eval_jaxpr/ppermute | solution.py:471
  270.0 14.5 %collective-permute-start.1 = (bf16[128,1536]{1,0:T(8,128)(2,1)S(1)}, bf16[128,1536]{1,0:T(8,128)(2,1)S(1)}, u32[]{:S(2)}, u32[]{:S(2)}) collective-permute-start(bf16[128,1536]{1,0:T(8,128)(2,1)S(1)} %add_convert_fusion.5), channel_id=1, source_target_pairs={{4,0},{5,1},{6,2},{7,3},{8,4},{9,5},{10,6},{11,7},{12,8},{13,9},{1... | collective-permute-start | bytes 1179656 | tf_op jit(solution)/shard_map/while/body/eval_jaxpr/ppermute | solution.py:471
  309.0 8.8 %collective-permute-start.3 = (bf16[16,1792]{1,0:T(8,128)(2,1)S(1)}, bf16[16,1792]{1,0:T(8,128)(2,1)S(1)}, u32[]{:S(2)}, u32[]{:S(2)}) collective-permute-start(bf16[16,1792]{1,0:T(8,128)(2,1)S(1)} %slice.41), channel_id=1, source_target_pairs={{4,0},{5,1},{6,2},{7,3},{8,4},{9,5},{10,6},{11,7},{12,8},{13,9},{1... | collective-permute-start | bytes 172040 | tf_op jit(solution)/shard_map/ppermute | solution.py:530
  346.4 1.1 copy-start.1
  354.7 4.7 copy-start.2
  355.7 24.0 %all-to-all-start.2 = ((bf16[4,2,49152]{2,1,0:T(2,128)(2,1)}), bf16[4,2,49152]{2,1,0:T(2,128)(2,1)S(1)}, u32[]{:S(2)}, u32[]{:S(2)}) async-start(bf16[4,2,49152]{2,1,0:T(2,128)(2,1)} %reshape.71), calls=%async_computation.2 | async-start | bytes 1572864 | tf_op jit(solution)/shard_map/all_to_all | solution.py:465
  366.1 17.1 %copy-start.6 = (f32[1,1792]{1,0:T(1,128)S(1)}, f32[1,1792]{1,0:T(1,128)}, u32[]{:S(2)}) copy-start(f32[1,1792]{1,0:T(1,128)} %get-tuple-element.121) | copy-start | bytes 21508
  366.1 17.2 %copy-start.7 = (f32[1,1536]{1,0:T(1,128)S(1)}, f32[1,1536]{1,0:T(1,128)}, u32[]{:S(2)}) copy-start(f32[1,1536]{1,0:T(1,128)} %get-tuple-element.125) | copy-start | bytes 18436
  366.1 17.2 %copy-start.15 = (f32[1,128]{1,0:T(1,128)S(1)}, f32[1,128]{1,0:T(1,128)}, u32[]{:S(2)}) copy-start(f32[1,128]{1,0:T(1,128)} %get-tuple-element.123) | copy-start | bytes 1540
  366.2 17.2 %copy-start.14 = (f32[1,128]{1,0:T(1,128)S(1)}, f32[1,128]{1,0:T(1,128)}, u32[]{:S(2)}) copy-start(f32[1,128]{1,0:T(1,128)} %get-tuple-element.122) | copy-start | bytes 1540
  366.2 17.2 %copy-start.13 = (f32[1,128]{1,0:T(1,128)S(1)}, f32[1,128]{1,0:T(1,128)}, u32[]{:S(2)}) copy-start(f32[1,128]{1,0:T(1,128)} %get-tuple-element.124) | copy-start | bytes 1540
  366.2 17.2 %copy-start.9 = (f32[1,768]{1,0:T(1,128)S(1)}, f32[1,768]{1,0:T(1,128)}, u32[]{:S(2)}) copy-start(f32[1,768]{1,0:T(1,128)} %get-tuple-element.118) | copy-start | bytes 9220
  366.2 17.2 %copy-start.3 = (f32[4,1792]{1,0:T(4,128)S(1)}, f32[4,1792]{1,0:T(4,128)}, u32[]{:S(2)}) copy-start(f32[4,1792]{1,0:T(4,128)} %get-tuple-element.120) | copy-start | bytes 86020
  379.7 57.6 %all-to-all-start.3 = ((bf16[4,2,49152]{2,1,0:T(2,128)(2,1)}), bf16[4,2,49152]{2,1,0:T(2,128)(2,1)S(1)}, u32[]{:S(2)}, u32[]{:S(2)}) async-start(bf16[4,2,49152]{2,1,0:T(2,128)(2,1)} %reshape.73), calls=%async_computation.3 | async-start | bytes 1572864 | tf_op jit(solution)/shard_map/all_to_all | solution.py:465
Sparse Core Ops, SparseCore 0:
  10.9 80.7 all-gather.4
  94.4 56.3 all-gather.2
  211.1 121.8 reduce-scatter.4
  346.6 154.4 reduce-scatter.6

commit v2 on v1

--- a/solution.py
+++ b/solution.py
@@ -28,7 +28,7 @@
     return max(t for t in range(16, most + 1, 16) if rows % t == 0)
 
 
-def fill_spread(e_ref, head_dim, heads):
+def fill_spread(e_ref, head_dim):
     channels = e_ref.shape[1]
     row = lax.broadcasted_iota(jnp.int32, (LANES, channels), 0)
     col = lax.broadcasted_iota(jnp.int32, (LANES, channels), 1)
@@ -78,9 +78,245 @@
         total = total + w_ref[k : k + 1, pl.ds(c0, cols)] * shifts[-1]
     return total, shifts
 
+MESH = pl.DeviceIdType.MESH
+HBM = pl.BlockSpec(memory_space=pl.ANY)
+VMEM = pl.BlockSpec(memory_space=pltpu.VMEM)
+
+
+def aligned(value, multiple):
+    return pl.multiple_of(value, multiple)
+
+
+def send(src, dst, send_sem, recv_sem, to):
+    copy = pltpu.make_async_remote_copy(
+        src_ref=src, dst_ref=dst, send_sem=send_sem, recv_sem=recv_sem, device_id=to, device_id_type=MESH
+    )
+    copy.start()
+    return copy
+
+
+def arrived(ref, sem):
+    pltpu.make_async_copy(ref, ref, sem).wait()
+
+
+class Place:
+    def __init__(self):
+        self.s, self.z = lax.axis_index("shard"), lax.axis_index("head")
+        s = self.s
+        self.core, self.cx, self.cy = s % 2, (s // 2) % 2, s // 4
+        self.s_core = s + 1 - 2 * self.core
+        self.s_x = s + 2 - 4 * self.cx
+        self.s_y = s + 4 - 8 * self.cy
+        self.s_diag = self.s_x + 4 - 8 * self.cy
+
+    def at(self, s=None, z=None):
+        return {"shard": self.s if s is None else s, "head": self.z if z is None else z}
+
+    def core_of(self, s):
+        return s + 1 - 2 * (s % 2)
+
+
+def greet(targets, count):
+    barrier = pltpu.get_barrier_semaphore()
+    for device, condition in targets:
+        if condition is None:
+            pl.semaphore_signal(barrier, inc=1, device_id=device, device_id_type=MESH)
+        else:
+
+            @pl.when(condition)
+            def _(device=device):
+                pl.semaphore_signal(barrier, inc=1, device_id=device, device_id_type=MESH)
+
+    pl.semaphore_wait(barrier, count)
+
+
+class Gather:
+    SEMS = [
+        pltpu.SemaphoreType.DMA((2, 4)),
+        pltpu.SemaphoreType.DMA((4,)),
+        pltpu.SemaphoreType.DMA((3, 4)),
+        pltpu.SemaphoreType.DMA((3, 4)),
+        pltpu.SemaphoreType.DMA((4, 4)),
+        pltpu.SemaphoreType.DMA((4, 4)),
+        pltpu.SemaphoreType.DMA,
+    ]
+
+    def __init__(self, place, own, full, sems):
+        self.p, self.own, self.full = place, own, full
+        self.z_send, self.z_recv, self.send, self.recv, self.c_send, self.c_recv, self.local = sems
+
+    def unit(self, s, z):
+        rows = self.own.shape[0]
+        return self.full.at[pl.ds(aligned((s * 4 + z) * rows, 8), rows), :]
+
+    def outward(self, src, z):
+        p = self.p
+        to = self.unit(p.s, z)
+        send(src, to, self.send.at[0, z], self.recv.at[0, z], p.at(s=p.s_x))
+        send(src, to, self.send.at[1, z], self.recv.at[1, z], p.at(s=p.s_y))
+        send(src, to, self.c_send.at[0, z], self.c_recv.at[0, z], p.at(s=p.s_core))
+
+    def start(self):
+        p = self.p
+        self.keep = pltpu.make_async_copy(self.own, self.unit(p.s, p.z), self.local)
+        self.keep.start()
+        to = self.unit(p.s, p.z)
+
+        @pl.when(p.z < 3)
+        def _():
+            send(self.own, to, self.z_send.at[0, p.z], self.z_recv.at[p.z], p.at(z=p.z + 1))
+
+        @pl.when(p.z > 0)
+        def _():
+            send(self.own, to, self.z_send.at[1, p.z], self.z_recv.at[p.z], p.at(z=p.z - 1))
+
+        self.outward(self.own, p.z)
+
+    def both_sides(self, k, act):
+        p = self.p
+        if k == 0:
+            act(p.z, None)
+            return
+
+        @pl.when(p.z >= k)
+        def _():
+            act(p.z - k, 0)
+
+        @pl.when(p.z + k <= 3)
+        def _():
+            act(p.z + k, 1)
+
+    def column(self, k):
+        p = self.p
+
+        def act(z, side):
+            unit = self.unit(p.s, z)
+            arrived(unit, self.z_recv.at[z])
+            if side == 0:
+
+                @pl.when(p.z < 3)
+                def _():
+                    send(unit, unit, self.z_send.at[0, z], self.z_recv.at[z], p.at(z=p.z + 1))
+
+            else:
+
+                @pl.when(p.z > 0)
+                def _():
+                    send(unit, unit, self.z_send.at[1, z], self.z_recv.at[z], p.at(z=p.z - 1))
+
+            self.outward(unit, z)
+
+        self.both_sides(k, act)
+
+    def sideways(self, k):
+        p = self.p
+
+        def act(z, side):
+            for axis, s in ((0, p.s_x), (1, p.s_y)):
+                unit = self.unit(s, z)
+                arrived(unit, self.recv.at[axis, z])
+                onward = p.s_y if axis == 0 else p.s_x
+                turn = z < 2 if axis == 0 else z >= 2
+
+                @pl.when(turn)
+                def _(unit=unit, onward=onward):
+                    send(unit, unit, self.send.at[2, z], self.recv.at[2, z], p.at(s=onward))
+
+                send(unit, unit, self.c_send.at[1 + axis, z], self.c_recv.at[1 + axis, z], p.at(s=p.s_core))
+
+        self.both_sides(k, act)
+
+    def diagonal(self, k):
+        p = self.p
+
+        def act(z, side):
+            unit = self.unit(p.s_diag, z)
+            arrived(unit, self.recv.at[2, z])
+            send(unit, unit, self.c_send.at[3, z], self.c_recv.at[3, z], p.at(s=p.s_core))
+
+        self.both_sides(k, act)
+
+    def steps(self):
+        todo = []
+        for k in range(1, 4):
+            todo.append(functools.partial(self.column, k))
+            todo.append(functools.partial(self.sideways, k - 1))
+            if k > 1:
+                todo.append(functools.partial(self.diagonal, k - 2))
+        todo.append(functools.partial(self.sideways, 3))
+        todo.append(functools.partial(self.diagonal, 2))
+        todo.append(functools.partial(self.diagonal, 3))
+        todo.append(self.others)
+        return todo
+
+    def others(self):
+        p = self.p
+        for column, s in enumerate((p.s, p.s_x, p.s_y, p.s_diag)):
+            for z in range(4):
+                arrived(self.unit(p.core_of(s), z), self.c_recv.at[column, z])
+        self.keep.wait()
+
+    def drain(self):
+        p = self.p
+        for z in range(4):
+            unit = self.unit(p.s, z)
+
+            @pl.when((p.z < 3) & (z <= p.z))
+            def _(unit=unit, z=z):
+                arrived(unit, self.z_send.at[0, z])
+
+            @pl.when((p.z > 0) & (z >= p.z))
+            def _(unit=unit, z=z):
+                arrived(unit, self.z_send.at[1, z])
+
+            for axis in range(3):
+                arrived(unit, self.send.at[axis, z])
+            for column in range(4):
+                arrived(unit, self.c_send.at[column, z])
+
+
+class Exchange:
+    SEMS = [pltpu.SemaphoreType.DMA((4,)), pltpu.SemaphoreType.DMA((4,)), pltpu.SemaphoreType.DMA]
+
+    def __init__(self, place, blocks, rows, offset, sems):
+        self.p, self.blocks, self.rows, self.offset = place, blocks, rows, offset
+        self.send, self.recv, self.local = sems
+
+    def part(self, z):
+        size = self.blocks.shape[1]
+        return self.rows.at[pl.ds(aligned(self.offset + z * size, 16), size), :]
+
+    def start(self):
+        p = self.p
+        self.keep = pltpu.make_async_copy(self.blocks.at[p.z], self.part(p.z), self.local)
+        self.keep.start()
+        for k in (1, 2, 3):
+            z = (p.z + k) % 4
+            send(self.blocks.at[z], self.part(p.z), self.send.at[z], self.recv.at[p.z], p.at(z=z))
+
+    def finish(self):
+        p = self.p
+        for k in (1, 2, 3):
+            z = (p.z + k) % 4
+            arrived(self.part(z), self.recv.at[z])
+        self.keep.wait()
+
+    def drain(self):
+        p = self.p
+        for k in (1, 2, 3):
+            z = (p.z + k) % 4
+            arrived(self.part(z), self.send.at[z])
+
 
 def project_kernel(tok, w_in, gain, conv_w, conv_b, dt_bias, a_log,
-                   normed, gate, raw, dt_raw, act, dt, cum, cum_t, loc, dec, e, state):
+                   normed, gate, raw, dt_raw, act, dt, cum, cum_t, loc, dec, e, state, between=()):
+    between = list(between)
+
+    def comm(count=1):
+        for _ in range(count):
+            if between:
+                between.pop(0)()
+
     ext, d = tok.shape
     inner = gate.shape[1]
     conv_ch = raw.shape[1]
@@ -89,7 +325,7 @@
     state_n = (conv_ch - inner) // 2
     length = ext - HALO
     chunks = length // CHUNK
-    fill_spread(e, inner // heads, heads)
+    fill_spread(e, inner // heads)
     dt_raw[...] = jnp.zeros_like(dt_raw)
     rt = tile_of(ext, 192)
     ct = 512
@@ -104,7 +340,7 @@
     lax.fori_loop(0, ext // 16, norm_rows, 0)
 
     def proj_rows(i, _):
-        rows = pl.ds(pl.multiple_of(i * rt, 16), rt)
+        rows = pl.ds(i * rt, rt)
         n = normed[rows, :]
 
         def gate_cols(j, _):
@@ -125,7 +361,9 @@
         dt_raw[rows, 0:heads] = last[:, conv_ch - inner :].astype(BF16).astype(F32)
         return 0
 
-    lax.fori_loop(0, ext // rt, proj_rows, 0)
+    for i in range(ext // rt):
+        proj_rows(i, 0)
+        comm(2)
 
     def conv_tile(i, _):
         r0 = pl.multiple_of(i * 64, 64)
@@ -138,7 +376,9 @@
 
         return lax.fori_loop(0, conv_ch // 256, conv_cols, 0)
 
-    lax.fori_loop(0, length // 64, conv_tile, 0)
+    for part in range(4):
+        lax.fori_loop(part * length // 256, (part + 1) * length // 256, conv_tile, 0)
+        comm()
 
     t_i = lax.broadcasted_iota(jnp.int32, (CHUNK, CHUNK), 0)
     s_i = lax.broadcasted_iota(jnp.int32, (CHUNK, CHUNK), 1)
@@ -166,6 +406,62 @@
 
     lax.fori_loop(0, chunks, chunk, 0)
     loc[chunks] = state[...]
+    comm(len(between))
+
+
+def gather_kernel(blocks, grads, w_in_own, w_out_own, gain, conv_w, conv_b, dt_bias, a_log,
+                  tok, og, w_in, w_out, normed, gate, raw, dt_raw, act, dt, cum, cum_t, loc, dec, e, state, *sems):
+    p = Place()
+    size = blocks.shape[1]
+    last = 7
+    targets = [(p.at(z=(p.z + k) % 4), None) for k in (1, 2, 3)]
+    targets += [(p.at(s=s), None) for s in (p.s_core, p.s_x, p.s_y)]
+    halo_out = (p.z == 3) & (p.s < last)
+    targets += [(p.at(s=p.s + 1, z=q), halo_out) for q in range(4)]
+    targets += [(p.at(s=p.s - 1, z=3), p.s > 0)]
+    greet(targets, 6 + jnp.where(p.s > 0, 1, 0) + jnp.where(halo_out, 4, 0))
+
+    n_g, n_x = len(Gather.SEMS), len(Exchange.SEMS)
+    first = Gather(p, w_in_own, w_in, sems[:n_g])
+    second = Gather(p, w_out_own, w_out, sems[n_g : 2 * n_g])
+    tokens = Exchange(p, blocks, tok, HALO, sems[2 * n_g : 2 * n_g + n_x])
+    cotangents = Exchange(p, grads, og, 0, sems[2 * n_g + n_x : 2 * n_g + 2 * n_x])
+    halo_send, halo_recv = sems[2 * n_g + 2 * n_x :]
+    halo = tok.at[0:HALO, :]
+    first.start()
+
+    @pl.when(halo_out)
+    def _():
+        for q in range(4):
+            send(blocks.at[q, size - HALO : size, :], halo, halo_send.at[q], halo_recv, p.at(s=p.s + 1, z=q))
+
+    tokens.start()
+    for step in first.steps():
+        step()
+    tokens.finish()
+
+    @pl.when(p.s > 0)
+    def _():
+        arrived(halo, halo_recv)
+
+    @pl.when(p.s == 0)
+    def _():
+        tok[0:HALO, :] = jnp.zeros((HALO, tok.shape[1]), tok.dtype)
+
+    second.start()
+    cotangents.start()
+    project_kernel(tok, w_in, gain, conv_w, conv_b, dt_bias, a_log, normed, gate, raw, dt_raw, act, dt, cum, cum_t, loc, dec,
+                   e, state, between=second.steps())
+    cotangents.finish()
+    first.drain()
+    second.drain()
+    tokens.drain()
+    cotangents.drain()
+
+    @pl.when(halo_out)
+    def _():
+        for q in range(4):
+            arrived(halo, halo_send.at[q])
 
 
 def mix_kernel(tok, og, w_out, gate, act, dt, cum, cum_t, loc, enter, gain, skip,
@@ -174,9 +470,7 @@
     state_n = loc.shape[1]
     chunks = length // CHUNK
     pairs = inner // LANES
-    fill_spread(e, skip.shape[1] // 1, 0) if False else None
-    head_dim = LANES // 2
-    fill_spread(e, head_dim, 0)
+    fill_spread(e, LANES // 2)
     t_i = lax.broadcasted_iota(jnp.int32, (CHUNK, CHUNK), 0)
     s_i = lax.broadcasted_iota(jnp.int32, (CHUNK, CHUNK), 1)
     causal = t_i >= s_i
@@ -267,7 +561,7 @@
     state_n = states.shape[1]
     chunks = length // CHUNK
     pairs = inner // LANES
-    fill_spread(e, LANES // 2, 0)
+    fill_spread(e, LANES // 2)
     s_i = lax.broadcasted_iota(jnp.int32, (CHUNK, CHUNK), 0)
     t_i = lax.broadcasted_iota(jnp.int32, (CHUNK, CHUNK), 1)
     causal = t_i >= s_i
@@ -413,17 +707,16 @@
     lax.fori_loop(0, d // 128, w_rows, 0)
 
 
-def vmem_call(kernel, outs, scratch, name):
-    spec = pl.BlockSpec(memory_space=pltpu.VMEM)
-
+def vmem_call(kernel, outs, scratch, name, in_hbm=(), sems=(), collective=None):
     def run(*args):
+        params = {} if collective is None else {"collective_id": collective, "has_side_effects": True}
         return pl.pallas_call(
             kernel,
             out_shape=[jax.ShapeDtypeStruct(s, t) for s, t in outs],
-            in_specs=[spec] * len(args),
-            out_specs=[spec] * len(outs),
-            scratch_shapes=[pltpu.VMEM(s, t) for s, t in scratch],
-            compiler_params=pltpu.CompilerParams(vmem_limit_bytes=VMEM_LIMIT),
+            in_specs=[HBM if i in in_hbm else VMEM for i in range(len(args))],
+            out_specs=[VMEM] * len(outs),
+            scratch_shapes=[pltpu.VMEM(s, t) for s, t in scratch] + list(sems),
+            compiler_params=pltpu.CompilerParams(vmem_limit_bytes=VMEM_LIMIT, **params),
             name=name,
         )(*args)
 
@@ -472,28 +765,35 @@
 
         return lax.fori_loop(0, ranges * parts - 1, hop, jnp.zeros(own.shape, BF16)).astype(F32)
 
-    full_in = lax.all_gather(w_in, both, axis=0, tiled=True)
-    full_out = lax.all_gather(w_out, both, axis=0, tiled=True)
-    tok = to_ranges(block_in)
-    og = to_ranges(out_grad)
-    tok = jnp.concatenate([lax.ppermute(tok[-HALO:], both, forth), tok], axis=0)
-
     pad = LANES - heads
     gain_in_row, gain_out_row, conv_b_row = gain_in[None], gain_out[None], conv_b[None]
     bias_row = jnp.pad(dt_bias, (0, pad))[None]
     rate_row = jnp.pad(a_log, (0, pad), constant_values=-1e30)[None]
     skip_row = jnp.repeat(d_skip, inner // heads)[None]
 
-    normed, gate, raw, dt_raw, act, dt, cum, cum_t, loc, dec = vmem_call(
-        project_kernel,
-        [
-            ((ext, d), BF16), ((ext, inner), BF16), ((ext, conv_ch), BF16), ((ext, LANES), F32), ((length, conv_ch), BF16),
-            ((length, LANES), F32), ((length, LANES), F32), ((chunks, LANES, CHUNK), F32),
-            ((chunks + 1, state_n, inner), F32), ((1, LANES), F32),
-        ],
-        [((2 * LANES, inner), BF16), ((state_n, inner), F32)],
-        "project",
-    )(tok, full_in, gain_in_row, conv_w, conv_b_row, bias_row, rate_row)
+    own_links = (ranges, groups, seqs) == (8, 4, 4)
+    project_outs = [
+        ((ext, d), BF16), ((ext, inner), BF16), ((ext, conv_ch), BF16), ((ext, LANES), F32), ((length, conv_ch), BF16),
+        ((length, LANES), F32), ((length, LANES), F32), ((chunks, LANES, CHUNK), F32),
+        ((chunks + 1, state_n, inner), F32), ((1, LANES), F32),
+    ]
+    project_scratch = [((2 * LANES, inner), BF16), ((state_n, inner), F32)]
+    if own_links:
+        shapes = [((ext, d), BF16), ((length, d), BF16), ((d, w_in.shape[1]), BF16), ((inner, d), BF16)]
+        tok, og, full_in, full_out, *made = vmem_call(
+            gather_kernel, shapes + project_outs, project_scratch, "gather", in_hbm=range(4),
+            sems=Gather.SEMS * 2 + Exchange.SEMS * 2 + [pltpu.SemaphoreType.DMA((4,)), pltpu.SemaphoreType.DMA], collective=0,
+        )(block_in, out_grad, w_in, w_out, gain_in_row, conv_w, conv_b_row, bias_row, rate_row)
+    else:
+        full_in = lax.all_gather(w_in, both, axis=0, tiled=True)
+        full_out = lax.all_gather(w_out, both, axis=0, tiled=True)
+        tok = to_ranges(block_in)
+        og = to_ranges(out_grad)
+        tok = jnp.concatenate([lax.ppermute(tok[-HALO:], both, forth), tok], axis=0)
+        made = vmem_call(project_kernel, project_outs, project_scratch, "project")(
+            tok, full_in, gain_in_row, conv_w, conv_b_row, bias_row, rate_row
+        )
+    normed, gate, raw, dt_raw, act, dt, cum, cum_t, loc, dec = made
 
     decay = jnp.repeat(jnp.exp(dec[0, :heads]), inner // heads)[None]
     enter = chain(loc[chunks], decay, forth)

time: 509 us -> 493 us (0.969)
  waiting for transfers between devices: 222 us -> 153 us
  Pallas kernels: 108 us -> 173 us
  starting transfers between devices: 76.9 us -> 64.5 us
    pallas_call x4, Pallas kernels: 108 us -> 173 us  [run(): pl.pallas_call(kernel, out_shape=[jax.ShapeDtypeStruct(s, t) for s, t in...]
    all_gather x2 -> x0, waiting for transfers between devices: 44.8 us -> none  [the longest x1 44.8 us: shards(): full_in = lax.all_gather(w_in, both, axis=0, tiled=True)]
    all_to_all x2 -> x0, waiting for transfers between devices: 22.9 us -> none  [to_ranges(): lax.all_to_all(array, 'head', split_axis=0, concat_axis=1, tiled=True)[0]]
    all_to_all x2 -> x0, starting transfers between devices: 9.85 us -> none  [to_ranges(): lax.all_to_all(array, 'head', split_axis=0, concat_axis=1, tiled=True)[0]]
    unnamed x5 -> x3, waiting for transfers between devices: 63.2 us -> 61.7 us
  transfers between devices with their start and end apart: 24 -> 19, of which waited for: 19 -> 17; matrix products, arithmetic and copies ran while one was open for 6% -> 5% of each run, Pallas kernels for 15% -> 10%
where the time goes in v2:
time: 493 us; the launch traced here: 492 us
  Pallas kernels  173 us (35%)
  waiting for transfers between devices  153 us (31%)
  starting transfers between devices  64.5 us (13%)
  blocking collectives  52.5 us (11%)
  local copies, waits for them, and re-layouts  20.2 us (4%)
  between operations  14.3 us (3%)
  other arithmetic  14.2 us (3%)
    pallas_call x4, Pallas kernels, run(): pl.pallas_call(kernel, out_shape=[jax.ShapeDtypeStruct(s, t) for s, t in...  173 us
    ppermute x14, waiting for transfers between devices, hop(): lax.ppermute((decay * before.astype(F32) + own).astype(BF16), both, route)  71.3 us
    unnamed x3, waiting for transfers between devices  61.7 us
    ppermute x14, starting transfers between devices, hop(): lax.ppermute((decay * before.astype(F32) + own).astype(BF16), both, route)  55.6 us
    psum x1, blocking collectives, shards(): lax.psum((g_gain_in[0], g_gain_out[0], g_conv_w, g_conv_b[0], g_bias[0, :...  52.5 us
    all_to_all x2, waiting for transfers between devices, to_blocks(): lax.all_to_all(array[None], 'head', split_axis=1, concat_axis=0, tiled=True)  12.5 us
    unnamed x2, other arithmetic  10.9 us
  transfers between devices with their start and end apart: 19, of which 17 were waited for; matrix products, arithmetic and copies ran while one was open for 5% of the time, Pallas kernels for 10%

profile of v2, /device:TPU:0, one launch (start us, length us, event | category | flops | bytes accessed | tf_op | source)
XLA Modules:
  0.0 492.1 jit_solution(721811927908987973)
XLA Ops:
  7.2 1.3 broadcast_in_dim.28.conv_b
  8.5 1.3 broadcast_in_dim.27.gain
  9.8 1.2 pad_bitcast_fusion
  11.0 88.6 %gather.1 = (bf16[528,768]{1,0:T(8,128)(2,1)}, bf16[512,768]{1,0:T(8,128)(2,1)}, bf16[768,3352]{1,0:T(8,128)(2,1)}, bf16[1536,768]{1,0:T(8,128)(2,1)}, bf16[528,...) custom-call(bf16[4,128,768]{2,1,0:T(8,128)(2,1)} %blocks.1, ...), custom_call_target="tpu_custom_call" | custom-call | tf_op jit(solution)/shard_map/gather/pallas_call | solution.py:713
  99.6 1.2 slice_bitcast_fusion
  100.8 0.6 exponential_bitcast_fusion
  101.5 57.6 %while.23 = (s32[]{:T(128)}, bf16[128,1536]{1,0:T(8,128)(2,1)S(1)}, f32[128,1536]{1,0:T(8,128)S(1)}, f32[24]{0:T(128)S(1)}, s32[]{:T(128)}) while((s32[]{:T(128)}, bf16[128,1536]{1,0:T(8,128)(2,1)S(1)}, f32[128,1536]{1,0:T(8,128)S(1)}, f32[24]{0:T(128)S(1)}, s32[]{:T(128)}) %tuple.46), condition=%wide.region_1.2_spmd.clone, body=%wide.region_0.1_spmd.clone.sunk | while | flops 786434 | bytes 3170501 | solution.py:766
  101.7 2.4 collective-permute-start
  104.1 1.3 collective-permute-done
  105.7 5.3 %collective-permute-start = (bf16[128,1536]{1,0:T(8,128)(2,1)S(1)}, bf16[128,1536]{1,0:T(8,128)(2,1)S(1)}, u32[]{:S(2)}, u32[]{:S(2)}) collective-permute-start(bf16[128,1536]{1,0:T(8,128)(2,1)S(1)} %add_convert_fusion.4), channel_id=1, source_target_pairs={{0,4},{1,5},{2,6},{3,7},{4,8},{5,9},{6,10},{7,11},{8,12},{9,13},{1... | collective-permute-start | bytes 1179656 | tf_op jit(solution)/shard_map/while/body/eval_jaxpr/ppermute | solution.py:764
  111.0 1.3 collective-permute-done
  112.5 7.8 %collective-permute-start = (bf16[128,1536]{1,0:T(8,128)(2,1)S(1)}, bf16[128,1536]{1,0:T(8,128)(2,1)S(1)}, u32[]{:S(2)}, u32[]{:S(2)}) collective-permute-start(bf16[128,1536]{1,0:T(8,128)(2,1)S(1)} %add_convert_fusion.4), channel_id=1, source_target_pairs={{0,4},{1,5},{2,6},{3,7},{4,8},{5,9},{6,10},{7,11},{8,12},{9,13},{1... | collective-permute-start | bytes 1179656 | tf_op jit(solution)/shard_map/while/body/eval_jaxpr/ppermute | solution.py:764
  120.3 1.3 collective-permute-done
  121.9 7.8 %collective-permute-start = (bf16[128,1536]{1,0:T(8,128)(2,1)S(1)}, bf16[128,1536]{1,0:T(8,128)(2,1)S(1)}, u32[]{:S(2)}, u32[]{:S(2)}) collective-permute-start(bf16[128,1536]{1,0:T(8,128)(2,1)S(1)} %add_convert_fusion.4), channel_id=1, source_target_pairs={{0,4},{1,5},{2,6},{3,7},{4,8},{5,9},{6,10},{7,11},{8,12},{9,13},{1... | collective-permute-start | bytes 1179656 | tf_op jit(solution)/shard_map/while/body/eval_jaxpr/ppermute | solution.py:764
  129.7 1.3 collective-permute-done
  131.2 7.8 %collective-permute-start = (bf16[128,1536]{1,0:T(8,128)(2,1)S(1)}, bf16[128,1536]{1,0:T(8,128)(2,1)S(1)}, u32[]{:S(2)}, u32[]{:S(2)}) collective-permute-start(bf16[128,1536]{1,0:T(8,128)(2,1)S(1)} %add_convert_fusion.4), channel_id=1, source_target_pairs={{0,4},{1,5},{2,6},{3,7},{4,8},{5,9},{6,10},{7,11},{8,12},{9,13},{1... | collective-permute-start | bytes 1179656 | tf_op jit(solution)/shard_map/while/body/eval_jaxpr/ppermute | solution.py:764
  139.0 1.3 collective-permute-done
  140.6 7.8 %collective-permute-start = (bf16[128,1536]{1,0:T(8,128)(2,1)S(1)}, bf16[128,1536]{1,0:T(8,128)(2,1)S(1)}, u32[]{:S(2)}, u32[]{:S(2)}) collective-permute-start(bf16[128,1536]{1,0:T(8,128)(2,1)S(1)} %add_convert_fusion.4), channel_id=1, source_target_pairs={{0,4},{1,5},{2,6},{3,7},{4,8},{5,9},{6,10},{7,11},{8,12},{9,13},{1... | collective-permute-start | bytes 1179656 | tf_op jit(solution)/shard_map/while/body/eval_jaxpr/ppermute | solution.py:764
  148.4 1.3 collective-permute-done
  149.9 7.8 %collective-permute-start = (bf16[128,1536]{1,0:T(8,128)(2,1)S(1)}, bf16[128,1536]{1,0:T(8,128)(2,1)S(1)}, u32[]{:S(2)}, u32[]{:S(2)}) collective-permute-start(bf16[128,1536]{1,0:T(8,128)(2,1)S(1)} %add_convert_fusion.4), channel_id=1, source_target_pairs={{0,4},{1,5},{2,6},{3,7},{4,8},{5,9},{6,10},{7,11},{8,12},{9,13},{1... | collective-permute-start | bytes 1179656 | tf_op jit(solution)/shard_map/while/body/eval_jaxpr/ppermute | solution.py:764
  157.7 1.3 collective-permute-done
  159.0 1.0 convert_element_type.26.enter
  160.1 0.7 broadcast_in_dim_reshape.7.skip
  160.7 0.6 broadcast_in_dim.32.gain
  161.3 33.7 %mix.1 = (bf16[512,768]{1,0:T(8,128)(2,1)}, bf16[512,1536]{1,0:T(8,128)(2,1)}, bf16[512,1536]{1,0:T(8,128)(2,1)}, f32[1536,768]{1,0:T(8,128)}, f32[1,1536]{1,0:T...) custom-call(bf16[528,768]{1,0:T(8,128)(2,1)} %get-tuple-element.100., ...), custom_call_target="tpu_custom_call" | custom-call | tf_op jit(solution)/shard_map/mix/pallas_call | solution.py:713
  195.1 73.0 %while.24 = (s32[]{:T(128)}, bf16[128,1536]{1,0:T(8,128)(2,1)S(1)}, f32[128,1536]{1,0:T(8,128)S(1)}, f32[24]{0:T(128)S(1)}, s32[]{:T(128)}) while((s32[]{:T(128)}, bf16[128,1536]{1,0:T(8,128)(2,1)S(1)}, f32[128,1536]{1,0:T(8,128)S(1)}, f32[24]{0:T(128)S(1)}, s32[]{:T(128)}) %tuple.56), condition=%wide.region_3.4_spmd.clone, body=%wide.region_2.3_spmd.clone.sunk | while | flops 786434 | bytes 3170501 | solution.py:766
  195.4 1.3 collective-permute-start.1
  196.7 7.7 %collective-permute-done.1 = bf16[128,1536]{1,0:T(8,128)(2,1)S(1)} collective-permute-done((bf16[128,1536]{1,0:T(8,128)(2,1)S(1)}, bf16[128,1536]{1,0:T(8,128)(2,1)S(1)}, u32[]{:S(2)}, u32[]{:S(2)}) %collective-permute-start.1) | collective-permute-done | bytes 393248 | tf_op jit(solution)/shard_map/while/body/eval_jaxpr/ppermute | solution.py:764
  204.6 1.3 collective-permute-start.1
  205.9 8.5 %collective-permute-done.1 = bf16[128,1536]{1,0:T(8,128)(2,1)S(1)} collective-permute-done((bf16[128,1536]{1,0:T(8,128)(2,1)S(1)}, bf16[128,1536]{1,0:T(8,128)(2,1)S(1)}, u32[]{:S(2)}, u32[]{:S(2)}) %collective-permute-start.1) | collective-permute-done | bytes 393248 | tf_op jit(solution)/shard_map/while/body/eval_jaxpr/ppermute | solution.py:764
  214.7 1.3 collective-permute-start.1
  216.0 7.8 %collective-permute-done.1 = bf16[128,1536]{1,0:T(8,128)(2,1)S(1)} collective-permute-done((bf16[128,1536]{1,0:T(8,128)(2,1)S(1)}, bf16[128,1536]{1,0:T(8,128)(2,1)S(1)}, u32[]{:S(2)}, u32[]{:S(2)}) %collective-permute-start.1) | collective-permute-done | bytes 393248 | tf_op jit(solution)/shard_map/while/body/eval_jaxpr/ppermute | solution.py:764
  224.1 1.3 collective-permute-start.1
  225.4 7.9 %collective-permute-done.1 = bf16[128,1536]{1,0:T(8,128)(2,1)S(1)} collective-permute-done((bf16[128,1536]{1,0:T(8,128)(2,1)S(1)}, bf16[128,1536]{1,0:T(8,128)(2,1)S(1)}, u32[]{:S(2)}, u32[]{:S(2)}) %collective-permute-start.1) | collective-permute-done | bytes 393248 | tf_op jit(solution)/shard_map/while/body/eval_jaxpr/ppermute | solution.py:764
  233.5 1.3 collective-permute-start.1
  234.8 8.7 %collective-permute-done.1 = bf16[128,1536]{1,0:T(8,128)(2,1)S(1)} collective-permute-done((bf16[128,1536]{1,0:T(8,128)(2,1)S(1)}, bf16[128,1536]{1,0:T(8,128)(2,1)S(1)}, u32[]{:S(2)}, u32[]{:S(2)}) %collective-permute-start.1) | collective-permute-done | bytes 393248 | tf_op jit(solution)/shard_map/while/body/eval_jaxpr/ppermute | solution.py:764
  243.7 1.3 collective-permute-start.1
  245.0 8.6 %collective-permute-done.1 = bf16[128,1536]{1,0:T(8,128)(2,1)S(1)} collective-permute-done((bf16[128,1536]{1,0:T(8,128)(2,1)S(1)}, bf16[128,1536]{1,0:T(8,128)(2,1)S(1)}, u32[]{:S(2)}, u32[]{:S(2)}) %collective-permute-start.1) | collective-permute-done | bytes 393248 | tf_op jit(solution)/shard_map/while/body/eval_jaxpr/ppermute | solution.py:764
  253.9 1.3 collective-permute-start.1
  255.2 12.9 %collective-permute-done.1 = bf16[128,1536]{1,0:T(8,128)(2,1)S(1)} collective-permute-done((bf16[128,1536]{1,0:T(8,128)(2,1)S(1)}, bf16[128,1536]{1,0:T(8,128)(2,1)S(1)}, u32[]{:S(2)}, u32[]{:S(2)}) %collective-permute-start.1) | collective-permute-done | bytes 393248 | tf_op jit(solution)/shard_map/while/body/eval_jaxpr/ppermute | solution.py:764
  268.1 1.0 convert_element_type.27.leaving
  269.1 22.9 %back.1 = (bf16[528,1792]{1,0:T(8,128)(2,1)}, f32[512,128]{1,0:T(8,128)}, f32[4,1792]{1,0:T(4,128)}, f32[1,1792]{1,0:T(1,128)}, f32[1,128]{1,0:T(1,128)}, /*index=5*/f32[1,128]{1,0:T(1,128)}) custom-call(bf16[528,1792]{1,0:T(8,128)(2,1)} %get-tuple-element.115.raw, f32[528,128]{1,0:T(8,128)} %get-tuple-element.116.dt_raw, ...), custom_call_target="tpu_custom_call" | custom-call | tf_op jit(solution)/shard_map/back/pallas_call | solution.py:713
  292.0 0.8 slice.37
  292.8 1.5 collective-permute-start.2
  294.2 7.3 %collective-permute-done.2 = bf16[16,1792]{1,0:T(8,128)(2,1)S(1)} collective-permute-done((bf16[16,1792]{1,0:T(8,128)(2,1)S(1)}, bf16[16,1792]{1,0:T(8,128)(2,1)S(1)}, u32[]{:S(2)}, u32[]{:S(2)}) %collective-permute-start.2) | collective-permute-done | bytes 57376 | tf_op jit(solution)/shard_map/ppermute | solution.py:830
  301.5 0.6 constant_dynamic-update-slice_fusion.d_pre
  302.2 28.0 %input.1 = (bf16[512,768]{1,0:T(8,128)(2,1)}, f32[768,3352]{1,0:T(8,128)}, f32[1,768]{1,0:T(1,128)}) custom-call(bf16[528,768]{1,0:T(8,128)(2,1)} %get-tuple-element.100.tok, bf16[512,768]{1,0:T(8,128)(2,1)} %get-tuple-element.101.og, bf16[528,768]{1,0:T(8,128)(2,1)} %get-tuple-element.112.normed, bf16[768,3352]{1,0:T(8,128)(2,1)} %get-tuple-element.113.w_in, ...), custom_call_target="tpu_custom_call" | custom-call | tf_op jit(solution)/shard_map/input/pallas_call | solution.py:713
  330.2 1.1 copy-done
  331.3 1.2 copy.31
  332.5 0.5 broadcast.26
  333.0 5.4 %reduce.5 = bf16[512,768]{1,0:T(8,128)(2,1)S(1)} reduce(bf16[512,1,768]{2,1,0:T(2,128)(2,1)S(1)} %bitcast.26, bf16[]{:T(256)} %broadcast.26), dimensions={1}, to_apply=%bitcast.25.reduce_sub_computation | reduce | bytes 1572866
  338.5 1.0 reshape.63
  339.5 3.8 all-to-all-start
  343.3 1.2 copy.30
  344.6 5.4 %reduce.6 = bf16[512,768]{1,0:T(8,128)(2,1)S(1)} reduce(bf16[512,1,768]{2,1,0:T(2,128)(2,1)S(1)} %bitcast.27, bf16[]{:T(256)} %broadcast.26), dimensions={1}, to_apply=%bitcast.24.reduce_sub_computation | reduce | bytes 1572866
  350.1 1.0 reshape.65
  351.1 12.5 %all-to-all-done = bf16[4,2,49152]{2,1,0:T(2,128)(2,1)S(1)} async-done(((bf16[4,2,49152]{2,1,0:T(2,128)(2,1)}), bf16[4,2,49152]{2,1,0:T(2,128)(2,1)S(1)}, u32[]{:S(2)}, u32[]{:S(2)}) %all-to-all-start) | async-done | bytes 786464 | tf_op jit(solution)/shard_map/all_to_all | solution.py:758
  363.6 3.5 all-to-all-start.1
  367.3 52.5 %all-reduce.3 = (f32[768]{0:T(1024)}, f32[4,1792]{1,0:T(4,128)}, f32[1792]{0:T(1024)}, f32[24]{0:T(128)}, f32[24]{0:T(128)}, /*index=5*/f32[24]{0:T(128)}, f32[1536]{0:T(1024)}) all-reduce(f32[768]{0:T(1024)S(1)} %reduce.2, f32[4,1792]{1,0:T(4,128)S(1)} %copy-done.2, ...), channel_id=1, replica_groups=mesh['shard'=8,'head'=4] {'shard','head'}, use_global_device_ids=true, to_apply=%region_4.5 | all-reduce | flops 11336 | bytes 90688 | tf_op jit(solution)/shard_map/psum | solution.py:841
  419.8 0.7 reshape.64
  420.6 1.0 copy.26
  421.5 0.7 reshape.66
  422.3 1.2 copy.27
  423.5 61.7 %reduce-scatter.7.cloned.1.call-done = f32[24,3352]{1,0:T(8,128)} async-done(((f32[768,3352]{1,0:T(8,128)}), f32[24,3352]{1,0:T(8,128)}) %reduce-scatter.7.cloned.1.call-update) | async-done | bytes 321808
  (78 shorter events, 3.7 us)
Async XLA Ops:
  7.2 416.4 %reduce-scatter.5.cloned.1.call-start = ((), (), s32[]{:S(2)}) async-start(), calls=%async_computation.4 | async-start | bytes 4866048 | tf_op jit(solution)/shard_map/reduce_scatter | solution.py:840
  101.4 58.5 %copy-start.7 = (f32[24]{0:T(128)S(1)}, f32[24]{0:T(128)}, u32[]{:S(2)}) copy-start(f32[24]{0:T(128)} %param.24) | copy-start | bytes 292
  101.5 59.3 %copy-start.3 = (f32[1536]{0:T(1024)S(1)}, f32[1536]{0:T(1024)}, u32[]{:S(2)}) copy-start(f32[1536]{0:T(1024)} %param.25) | copy-start | bytes 18436
  101.7 3.7 collective-permute-start
  105.7 6.6 %collective-permute-start = (bf16[128,1536]{1,0:T(8,128)(2,1)S(1)}, bf16[128,1536]{1,0:T(8,128)(2,1)S(1)}, u32[]{:S(2)}, u32[]{:S(2)}) collective-permute-start(bf16[128,1536]{1,0:T(8,128)(2,1)S(1)} %add_convert_fusion.4), channel_id=1, source_target_pairs={{0,4},{1,5},{2,6},{3,7},{4,8},{5,9},{6,10},{7,11},{8,12},{9,13},{1... | collective-permute-start | bytes 1179656 | tf_op jit(solution)/shard_map/while/body/eval_jaxpr/ppermute | solution.py:764
  112.5 9.1 %collective-permute-start = (bf16[128,1536]{1,0:T(8,128)(2,1)S(1)}, bf16[128,1536]{1,0:T(8,128)(2,1)S(1)}, u32[]{:S(2)}, u32[]{:S(2)}) collective-permute-start(bf16[128,1536]{1,0:T(8,128)(2,1)S(1)} %add_convert_fusion.4), channel_id=1, source_target_pairs={{0,4},{1,5},{2,6},{3,7},{4,8},{5,9},{6,10},{7,11},{8,12},{9,13},{1... | collective-permute-start | bytes 1179656 | tf_op jit(solution)/shard_map/while/body/eval_jaxpr/ppermute | solution.py:764
  121.9 9.1 %collective-permute-start = (bf16[128,1536]{1,0:T(8,128)(2,1)S(1)}, bf16[128,1536]{1,0:T(8,128)(2,1)S(1)}, u32[]{:S(2)}, u32[]{:S(2)}) collective-permute-start(bf16[128,1536]{1,0:T(8,128)(2,1)S(1)} %add_convert_fusion.4), channel_id=1, source_target_pairs={{0,4},{1,5},{2,6},{3,7},{4,8},{5,9},{6,10},{7,11},{8,12},{9,13},{1... | collective-permute-start | bytes 1179656 | tf_op jit(solution)/shard_map/while/body/eval_jaxpr/ppermute | solution.py:764
  131.2 9.1 %collective-permute-start = (bf16[128,1536]{1,0:T(8,128)(2,1)S(1)}, bf16[128,1536]{1,0:T(8,128)(2,1)S(1)}, u32[]{:S(2)}, u32[]{:S(2)}) collective-permute-start(bf16[128,1536]{1,0:T(8,128)(2,1)S(1)} %add_convert_fusion.4), channel_id=1, source_target_pairs={{0,4},{1,5},{2,6},{3,7},{4,8},{5,9},{6,10},{7,11},{8,12},{9,13},{1... | collective-permute-start | bytes 1179656 | tf_op jit(solution)/shard_map/while/body/eval_jaxpr/ppermute | solution.py:764
  140.6 9.1 %collective-permute-start = (bf16[128,1536]{1,0:T(8,128)(2,1)S(1)}, bf16[128,1536]{1,0:T(8,128)(2,1)S(1)}, u32[]{:S(2)}, u32[]{:S(2)}) collective-permute-start(bf16[128,1536]{1,0:T(8,128)(2,1)S(1)} %add_convert_fusion.4), channel_id=1, source_target_pairs={{0,4},{1,5},{2,6},{3,7},{4,8},{5,9},{6,10},{7,11},{8,12},{9,13},{1... | collective-permute-start | bytes 1179656 | tf_op jit(solution)/shard_map/while/body/eval_jaxpr/ppermute | solution.py:764
  149.9 9.1 %collective-permute-start = (bf16[128,1536]{1,0:T(8,128)(2,1)S(1)}, bf16[128,1536]{1,0:T(8,128)(2,1)S(1)}, u32[]{:S(2)}, u32[]{:S(2)}) collective-permute-start(bf16[128,1536]{1,0:T(8,128)(2,1)S(1)} %add_convert_fusion.4), channel_id=1, source_target_pairs={{0,4},{1,5},{2,6},{3,7},{4,8},{5,9},{6,10},{7,11},{8,12},{9,13},{1... | collective-permute-start | bytes 1179656 | tf_op jit(solution)/shard_map/while/body/eval_jaxpr/ppermute | solution.py:764
  195.0 290.2 %reduce-scatter.7.cloned.1.call-start = ((), (), s32[]{:S(2)}) async-start(), calls=%async_computation.5 | async-start | bytes 10948608
  195.4 9.0 %collective-permute-start.1 = (bf16[128,1536]{1,0:T(8,128)(2,1)S(1)}, bf16[128,1536]{1,0:T(8,128)(2,1)S(1)}, u32[]{:S(2)}, u32[]{:S(2)}) collective-permute-start(bf16[128,1536]{1,0:T(8,128)(2,1)S(1)} %add_convert_fusion.5), channel_id=1, source_target_pairs={{4,0},{5,1},{6,2},{7,3},{8,4},{9,5},{10,6},{11,7},{12,8},{13,9},{1... | collective-permute-start | bytes 1179656 | tf_op jit(solution)/shard_map/while/body/eval_jaxpr/ppermute | solution.py:764
  204.6 9.8 %collective-permute-start.1 = (bf16[128,1536]{1,0:T(8,128)(2,1)S(1)}, bf16[128,1536]{1,0:T(8,128)(2,1)S(1)}, u32[]{:S(2)}, u32[]{:S(2)}) collective-permute-start(bf16[128,1536]{1,0:T(8,128)(2,1)S(1)} %add_convert_fusion.5), channel_id=1, source_target_pairs={{4,0},{5,1},{6,2},{7,3},{8,4},{9,5},{10,6},{11,7},{12,8},{13,9},{1... | collective-permute-start | bytes 1179656 | tf_op jit(solution)/shard_map/while/body/eval_jaxpr/ppermute | solution.py:764
  214.7 9.1 %collective-permute-start.1 = (bf16[128,1536]{1,0:T(8,128)(2,1)S(1)}, bf16[128,1536]{1,0:T(8,128)(2,1)S(1)}, u32[]{:S(2)}, u32[]{:S(2)}) collective-permute-start(bf16[128,1536]{1,0:T(8,128)(2,1)S(1)} %add_convert_fusion.5), channel_id=1, source_target_pairs={{4,0},{5,1},{6,2},{7,3},{8,4},{9,5},{10,6},{11,7},{12,8},{13,9},{1... | collective-permute-start | bytes 1179656 | tf_op jit(solution)/shard_map/while/body/eval_jaxpr/ppermute | solution.py:764
  224.1 9.2 %collective-permute-start.1 = (bf16[128,1536]{1,0:T(8,128)(2,1)S(1)}, bf16[128,1536]{1,0:T(8,128)(2,1)S(1)}, u32[]{:S(2)}, u32[]{:S(2)}) collective-permute-start(bf16[128,1536]{1,0:T(8,128)(2,1)S(1)} %add_convert_fusion.5), channel_id=1, source_target_pairs={{4,0},{5,1},{6,2},{7,3},{8,4},{9,5},{10,6},{11,7},{12,8},{13,9},{1... | collective-permute-start | bytes 1179656 | tf_op jit(solution)/shard_map/while/body/eval_jaxpr/ppermute | solution.py:764
  233.5 10.0 %collective-permute-start.1 = (bf16[128,1536]{1,0:T(8,128)(2,1)S(1)}, bf16[128,1536]{1,0:T(8,128)(2,1)S(1)}, u32[]{:S(2)}, u32[]{:S(2)}) collective-permute-start(bf16[128,1536]{1,0:T(8,128)(2,1)S(1)} %add_convert_fusion.5), channel_id=1, source_target_pairs={{4,0},{5,1},{6,2},{7,3},{8,4},{9,5},{10,6},{11,7},{12,8},{13,9},{1... | collective-permute-start | bytes 1179656 | tf_op jit(solution)/shard_map/while/body/eval_jaxpr/ppermute | solution.py:764
  243.7 9.9 %collective-permute-start.1 = (bf16[128,1536]{1,0:T(8,128)(2,1)S(1)}, bf16[128,1536]{1,0:T(8,128)(2,1)S(1)}, u32[]{:S(2)}, u32[]{:S(2)}) collective-permute-start(bf16[128,1536]{1,0:T(8,128)(2,1)S(1)} %add_convert_fusion.5), channel_id=1, source_target_pairs={{4,0},{5,1},{6,2},{7,3},{8,4},{9,5},{10,6},{11,7},{12,8},{13,9},{1... | collective-permute-start | bytes 1179656 | tf_op jit(solution)/shard_map/while/body/eval_jaxpr/ppermute | solution.py:764
  253.9 14.2 %collective-permute-start.1 = (bf16[128,1536]{1,0:T(8,128)(2,1)S(1)}, bf16[128,1536]{1,0:T(8,128)(2,1)S(1)}, u32[]{:S(2)}, u32[]{:S(2)}) collective-permute-start(bf16[128,1536]{1,0:T(8,128)(2,1)S(1)} %add_convert_fusion.5), channel_id=1, source_target_pairs={{4,0},{5,1},{6,2},{7,3},{8,4},{9,5},{10,6},{11,7},{12,8},{13,9},{1... | collective-permute-start | bytes 1179656 | tf_op jit(solution)/shard_map/while/body/eval_jaxpr/ppermute | solution.py:764
  292.8 8.8 %collective-permute-start.2 = (bf16[16,1792]{1,0:T(8,128)(2,1)S(1)}, bf16[16,1792]{1,0:T(8,128)(2,1)S(1)}, u32[]{:S(2)}, u32[]{:S(2)}) collective-permute-start(bf16[16,1792]{1,0:T(8,128)(2,1)S(1)} %slice.37), channel_id=1, source_target_pairs={{4,0},{5,1},{6,2},{7,3},{8,4},{9,5},{10,6},{11,7},{12,8},{13,9},{1... | collective-permute-start | bytes 172040 | tf_op jit(solution)/shard_map/ppermute | solution.py:830
  330.2 1.1 copy-start
  339.5 3.9 copy-start.1
  339.5 24.1 %all-to-all-start = ((bf16[4,2,49152]{2,1,0:T(2,128)(2,1)}), bf16[4,2,49152]{2,1,0:T(2,128)(2,1)S(1)}, u32[]{:S(2)}, u32[]{:S(2)}) async-start(bf16[4,2,49152]{2,1,0:T(2,128)(2,1)} %reshape.63), calls=%async_computation | async-start | bytes 1572864 | tf_op jit(solution)/shard_map/all_to_all | solution.py:758
  350.0 17.1 %copy-start.4 = (f32[1,1792]{1,0:T(1,128)S(1)}, f32[1,1792]{1,0:T(1,128)}, u32[]{:S(2)}) copy-start(f32[1,1792]{1,0:T(1,128)} %get-tuple-element.129) | copy-start | bytes 21508
  350.0 17.1 %copy-start.5 = (f32[1,1536]{1,0:T(1,128)S(1)}, f32[1,1536]{1,0:T(1,128)}, u32[]{:S(2)}) copy-start(f32[1,1536]{1,0:T(1,128)} %get-tuple-element.133) | copy-start | bytes 18436
  350.0 17.2 %copy-start.10 = (f32[1,128]{1,0:T(1,128)S(1)}, f32[1,128]{1,0:T(1,128)}, u32[]{:S(2)}) copy-start(f32[1,128]{1,0:T(1,128)} %get-tuple-element.131) | copy-start | bytes 1540
  350.0 17.2 %copy-start.9 = (f32[1,128]{1,0:T(1,128)S(1)}, f32[1,128]{1,0:T(1,128)}, u32[]{:S(2)}) copy-start(f32[1,128]{1,0:T(1,128)} %get-tuple-element.130) | copy-start | bytes 1540
  350.0 17.2 %copy-start.8 = (f32[1,128]{1,0:T(1,128)S(1)}, f32[1,128]{1,0:T(1,128)}, u32[]{:S(2)}) copy-start(f32[1,128]{1,0:T(1,128)} %get-tuple-element.132) | copy-start | bytes 1540
  350.0 17.2 %copy-start.6 = (f32[1,768]{1,0:T(1,128)S(1)}, f32[1,768]{1,0:T(1,128)}, u32[]{:S(2)}) copy-start(f32[1,768]{1,0:T(1,128)} %get-tuple-element.126) | copy-start | bytes 9220
  350.1 17.2 %copy-start.2 = (f32[4,1792]{1,0:T(4,128)S(1)}, f32[4,1792]{1,0:T(4,128)}, u32[]{:S(2)}) copy-start(f32[4,1792]{1,0:T(4,128)} %get-tuple-element.128) | copy-start | bytes 86020
  363.6 58.0 %all-to-all-start.1 = ((bf16[4,2,49152]{2,1,0:T(2,128)(2,1)}), bf16[4,2,49152]{2,1,0:T(2,128)(2,1)S(1)}, u32[]{:S(2)}, u32[]{:S(2)}) async-start(bf16[4,2,49152]{2,1,0:T(2,128)(2,1)} %reshape.65), calls=%async_computation.1 | async-start | bytes 1572864 | tf_op jit(solution)/shard_map/all_to_all | solution.py:758
Sparse Core Ops, SparseCore 0:
  195.2 123.4 reduce-scatter.4
  330.3 154.8 reduce-scatter.6
